TPU v7x, 32 devices: a whole 2x2x4 slice. The times are simulated.
32 devices in a mesh: tensor: 2 (over x), dp: 16 (over z, y, core).
Axes of the slice: x: 2, y: 2, z: 4, core: 2. Of those that a mesh axis runs over, the one named last changes fastest.
Arguments:
- tokens: bfloat16 [2048, 8192], P('dp', 'tensor'), may hold values from -6 to 6
- projection_weights: bfloat16 [2, 8192, 256], P(None, None, 'tensor'), may hold values from -0.0625 to 0.0625
- head_cotangent: bfloat16 [2, 2048, 256], P(None, 'dp', 'tensor'), may hold values from -6 to 6
- frequencies: int32 [2, 1024], replicated, may hold values from 0 to 8191, as said below
- sign_bits: int32 [2, 8192], replicated, may hold values 0 or 1
- first_moment: float32 [2, 1024, 256], P(None, 'dp', 'tensor'), may hold values from -6 to 6
- second_moment: float32 [2, 1024, 256], P(None, 'dp', 'tensor'), may hold values from 0.2 to 2
Outputs:
- input_gradient: bfloat16 [2048, 8192], P('dp', 'tensor')
- new_first: float32 [2, 1024, 256], P(None, 'dp', 'tensor')
- new_second: float32 [2, 1024, 256], P(None, 'dp', 'tensor')
- full_direction: bfloat16 [2, 8192, 256], P(None, 'dp', 'tensor')
Inputs may be any that keep to these rules, and one draw needn't show every extreme that they name: Each row holds 1024 different frequencies, and 0 is one of them.
All inputs are finite; a program needn't handle non-finite values.
Results may differ from a plain program's by a relative error of at most 0.013.
Values may be sent and summed in bfloat16 or wider, within the bound.
A program may use at most 64 MiB of HBM per device.

v0:
```python
import functools
import math

import jax
import jax.numpy as jnp
from jax import lax
from jax.experimental import pallas as pl
from jax.experimental.pallas import tpu as pltpu
from jax.sharding import PartitionSpec as P

first_fix = 1.0 - 0.9**10
second_fix = 1.0 - 0.95**10
epsilon = 1e-08


def trig(phase, width):
    phase = phase % (4 * width)
    quarter = (phase + width // 2) // width
    x = (phase - quarter * width).astype(jnp.float32) * (math.pi / (2 * width))
    y = x * x
    c = 1.0 + y * (-0.5 + y * (1 / 24 + y * (-1 / 720 + y * (1 / 40320 - y * (1 / 3628800)))))
    s = x * (1.0 + y * (-1 / 6 + y * (1 / 120 + y * (-1 / 5040 + y * (1 / 362880)))))
    quarter = quarter % 4
    odd = quarter % 2 == 1
    cosine = jnp.where(odd, s, c) * jnp.where((quarter == 1) | (quarter == 2), -1.0, 1.0)
    sine = jnp.where(odd, c, s) * jnp.where(quarter >= 2, -1.0, 1.0)
    return cosine, sine


def step_kernel(
    low_rows, chunk, token_count,
    tok_ref, w_ref, hc_ref, sign_ref, back_sign_ref, ca_ref, sa_ref, cb_ref, sb_ref, ra_ref, rb_ref,
    first_ref, second_ref,
    grad_ref, new_first_ref, new_second_ref, full_ref,
    acc, hc_all, tg_send, tg_recv, low_send, low_recv, part, x_send, x_recv, dirs, back_basis,
    hc_sems, tg_sems, low_sems, x_sems, dir_sems,
):
    rank = acc.shape[2]
    rows, lw = tok_ref.shape
    groups = chunk // low_rows
    n_dp, n_t, _, own, cols = low_send.shape
    me_t, me_d = lax.axis_index("tensor"), lax.axis_index("dp")

    def remote(src, dst, sems, slot, tensor, dp):
        return pltpu.make_async_remote_copy(
            src_ref=src,
            dst_ref=dst,
            send_sem=sems.at[0, slot],
            recv_sem=sems.at[1, slot],
            device_id={"tensor": tensor, "dp": dp},
            device_id_type=pl.DeviceIdType.MESH,
        )

    def peer_t(s):
        return lax.rem(me_t + s, n_t)

    def peer_d(s):
        return lax.rem(me_d + s, n_dp)

    barrier = pltpu.get_barrier_semaphore()

    def greet_t(s, carry):
        pl.semaphore_signal(
            barrier, inc=1, device_id={"tensor": peer_t(s), "dp": me_d},
            device_id_type=pl.DeviceIdType.MESH,
        )
        return carry

    def greet_d(s, carry):
        pl.semaphore_signal(
            barrier, inc=1, device_id={"tensor": me_t, "dp": peer_d(s)},
            device_id_type=pl.DeviceIdType.MESH,
        )
        return carry

    lax.fori_loop(1, n_t, greet_t, 0)
    lax.fori_loop(1, n_dp, greet_d, 0)
    pl.semaphore_wait(barrier, n_t + n_dp - 2)

    def hc_copy(s):
        return remote(hc_ref, hc_all.at[me_t], hc_sems, s, peer_t(s), me_d)

    def tg_copy(s):
        return remote(tg_send.at[s - 1], tg_recv.at[s - 1], tg_sems, s, peer_t(s), me_d)

    def low_copy(s):
        return remote(low_send.at[peer_d(s)], low_recv.at[s - 1], low_sems, s, me_t, peer_d(s))

    def x_copy(s):
        return remote(x_send.at[peer_t(s)], x_recv.at[s - 1], x_sems, s, peer_t(s), me_d)

    def dir_copy(s):
        return remote(dirs.at[me_d], dirs.at[me_d], dir_sems, s, me_t, peer_d(s))

    def each(count, act):
        def body(s, carry):
            act(s)
            return carry

        lax.fori_loop(1, count, body, 0)

    each(n_t, lambda s: hc_copy(s).start())
    hc_all[pl.ds(me_t, 1)] = hc_ref[...][None]
    wide = min(512, lw)

    def partial(t, j):
        total = 0.0
        for m in range(2):
            w = w_ref[m, pl.ds(pl.multiple_of(t * lw + j * wide, wide), wide), :]
            total = total + lax.dot_general(
                hc_ref[m], w, (((1,), (1,)), ((), ())), preferred_element_type=jnp.float32
            )
        return total.astype(jnp.bfloat16)

    def send_half(s):
        def tile(j, carry):
            tg_send[s - 1, :, pl.ds(pl.multiple_of(j * wide, wide), wide)] = partial(peer_t(s), j)
            return carry

        lax.fori_loop(0, lw // wide, tile, 0)
        tg_copy(s).start()

    each(n_t, send_half)
    acc[...] = jnp.zeros_like(acc)

    def tables(a_ref, b_ref, row, ks):
        row = pl.ds(row, 1)
        return (a_ref[row, ks] * cb_ref[:, ks] - b_ref[row, ks] * sb_ref[:, ks]).astype(jnp.bfloat16)

    def step(h, carry):
        columns = pl.ds(pl.multiple_of(h * chunk, chunk), chunk)
        tok = tok_ref[:, columns]
        for m in range(2):
            ks = slice(m * rank, (m + 1) * rank)
            parts = [tables(ca_ref, sa_ref, h * groups + g, ks) for g in range(groups)]
            basis = jnp.concatenate(parts, axis=0) if groups > 1 else parts[0]
            signed = tok * sign_ref[pl.ds(m, 1), columns].astype(jnp.bfloat16)
            acc[m] += jnp.dot(signed, basis, preferred_element_type=jnp.float32)
        return carry

    lax.fori_loop(0, lw // chunk, step, 0)
    each(n_t, lambda s: hc_copy(s).wait_recv())
    for m in range(2):
        heads = jnp.concatenate([hc_all[t, m] for t in range(n_t)], axis=1)
        low = lax.dot_general(
            acc[m].astype(jnp.bfloat16),
            heads,
            (((0,), (0,)), ((), ())),
            preferred_element_type=jnp.float32,
        ).astype(jnp.bfloat16)
        for t in range(n_t):
            low_send[:, t, m] = low[:, t * cols : (t + 1) * cols].reshape(n_dp, own, cols)
    each(n_dp, lambda s: low_copy(s).start())

    def own_tile(j, carry):
        grad_ref[:, pl.ds(pl.multiple_of(j * wide, wide), wide)] = partial(me_t, j)
        return carry

    lax.fori_loop(0, lw // wide, own_tile, 0)

    def back_rows(h, carry):
        for m in range(2):
            ks = slice(m * rank, (m + 1) * rank)
            place = pl.ds(pl.multiple_of(h * low_rows, low_rows), low_rows)
            back_basis[m, place, :] = tables(ra_ref, rb_ref, h, ks)
        return carry

    lax.fori_loop(0, back_basis.shape[1] // low_rows, back_rows, 0)
    part[...] = low_send[pl.ds(me_d, 1)][0].astype(jnp.float32)

    def add(s):
        low_copy(s).wait_recv()
        part[...] += low_recv[pl.ds(s - 1, 1)][0].astype(jnp.float32)

    each(n_dp, add)
    x_send[...] = part[...].astype(jnp.bfloat16)
    each(n_t, lambda s: x_copy(s).start())
    total = part[pl.ds(me_t, 1)][0]
    each(n_t, lambda s: x_copy(s).wait_recv())
    for s in range(1, n_t):
        total = total + x_recv[s - 1].astype(jnp.float32)
    gradient = total / math.sqrt(token_count)
    new_first = 0.9 * first_ref[...] + 0.1 * gradient
    new_second = 0.95 * second_ref[...] + 0.05 * gradient * gradient
    direction = new_first / first_fix / (jnp.sqrt(new_second / second_fix) + epsilon)
    dirs[pl.ds(me_d, 1)] = direction.astype(jnp.bfloat16)[None]
    each(n_dp, lambda s: dir_copy(s).start())
    new_first_ref[...] = new_first
    new_second_ref[...] = new_second
    each(n_t, lambda s: tg_copy(s).wait_recv())

    def finish(j, carry):
        place = pl.ds(pl.multiple_of(j * wide, wide), wide)
        summed = grad_ref[:, place].astype(jnp.float32)
        for s in range(1, n_t):
            summed = summed + tg_recv[s - 1, :, place].astype(jnp.float32)
        grad_ref[:, place] = summed.astype(jnp.bfloat16)
        return carry

    lax.fori_loop(0, lw // wide, finish, 0)

    def dir_arrival(s):
        source = lax.rem(me_d + n_dp - s, n_dp)
        remote(dirs.at[source], dirs.at[source], dir_sems, s, me_t, source).wait_recv()

    each(n_dp, dir_arrival)
    for m in range(2):
        product = jnp.dot(
            back_basis[m],
            dirs[:, m].reshape(rank, cols),
            preferred_element_type=jnp.float32,
        )
        full_ref[m] = (product * back_sign_ref[m]).astype(jnp.bfloat16)
    each(n_t, lambda s: hc_copy(s).wait_send())
    each(n_t, lambda s: tg_copy(s).wait_send())
    each(n_dp, lambda s: low_copy(s).wait_send())
    each(n_t, lambda s: x_copy(s).wait_send())
    each(n_dp, lambda s: dir_copy(s).wait_send())


def shards(
    tokens, projection_weights, head_cotangent, frequencies, sign_bits, first_moment, second_moment
):
    rows, local_width = tokens.shape
    n_tensor, n_dp = lax.axis_size("tensor"), lax.axis_size("dp")
    width = local_width * n_tensor
    token_count = rows * n_dp
    rank = frequencies.shape[1]
    own, cols = first_moment.shape[1], first_moment.shape[2]
    own_rows = projection_weights.shape[1] // n_dp
    low_rows = min(128, own_rows)
    chunk = min(256, local_width)
    me_t, me_d = lax.axis_index("tensor"), lax.axis_index("dp")
    offset = me_t * local_width
    row_offset = me_d * own_rows

    f = frequencies.reshape(1, 2 * rank)
    scale = jnp.where(f == 0, math.sqrt(1.0 / width), math.sqrt(2.0 / width)).astype(jnp.float32)
    cb, sb = trig((2 * lax.iota(jnp.int32, low_rows)[:, None] + 1) * f, width)
    hi = offset + low_rows * lax.iota(jnp.int32, local_width // low_rows)
    ca, sa = trig(2 * hi[:, None] * f, width)
    ca, sa = ca * scale, sa * scale
    hi_b = row_offset + low_rows * lax.iota(jnp.int32, own_rows // low_rows)
    ra, rb = trig(2 * hi_b[:, None] * f, width)
    ra, rb = ra * scale, rb * scale
    signs = (2 * sign_bits - 1).astype(jnp.float32)
    my_signs = lax.dynamic_slice_in_dim(signs, offset, local_width, 1)

    back_signs = lax.dynamic_slice_in_dim(signs, row_offset, own_rows, 1)[:, :, None]
    back_signs = jnp.broadcast_to(back_signs, (2, own_rows, cols))

    vmem = pl.BlockSpec(memory_space=pltpu.VMEM)
    bf16, f32 = jnp.bfloat16, jnp.float32
    pair = pltpu.SemaphoreType.DMA
    return pl.pallas_call(
        functools.partial(step_kernel, low_rows, chunk, token_count),
        out_shape=(
            jax.ShapeDtypeStruct((rows, local_width), bf16),
            jax.ShapeDtypeStruct((2, own, cols), f32),
            jax.ShapeDtypeStruct((2, own, cols), f32),
            jax.ShapeDtypeStruct((2, own_rows, cols), bf16),
        ),
        in_specs=[vmem] * 13,
        out_specs=(vmem,) * 4,
        scratch_shapes=[
            pltpu.VMEM((2, rows, rank), f32),
            pltpu.VMEM((n_tensor, 2, rows, cols), bf16),
            pltpu.VMEM((n_tensor - 1, rows, local_width), bf16),
            pltpu.VMEM((n_tensor - 1, rows, local_width), bf16),
            pltpu.VMEM((n_dp, n_tensor, 2, own, cols), bf16),
            pltpu.VMEM((n_dp - 1, n_tensor, 2, own, cols), bf16),
            pltpu.VMEM((n_tensor, 2, own, cols), f32),
            pltpu.VMEM((n_tensor, 2, own, cols), bf16),
            pltpu.VMEM((n_tensor - 1, 2, own, cols), bf16),
            pltpu.VMEM((n_dp, 2, own, cols), bf16),
            pltpu.VMEM((2, own_rows, rank), bf16),
            pair((2, n_tensor)),
            pair((2, n_tensor)),
            pair((2, n_dp)),
            pair((2, n_tensor)),
            pair((2, n_dp)),
        ],
        compiler_params=pltpu.CompilerParams(
            collective_id=0, has_side_effects=True, vmem_limit_bytes=56 * 1024 * 1024
        ),
    )(
        tokens, projection_weights, head_cotangent, my_signs, back_signs,
        ca, sa, cb, sb, ra, rb, first_moment, second_moment,
    )


def solution(mesh):
    in_specs = (
        P("dp", "tensor"),
        P(None, None, "tensor"),
        P(None, "dp", "tensor"),
        P(),
        P(),
        P(None, "dp", "tensor"),
        P(None, "dp", "tensor"),
    )
    out_specs = (
        P("dp", "tensor"),
        P(None, "dp", "tensor"),
        P(None, "dp", "tensor"),
        P(None, "dp", "tensor"),
    )
    return jax.shard_map(shards, mesh=mesh, in_specs=in_specs, out_specs=out_specs, check_vma=False)
```

profile of v0, /device:TPU:21, one launch (start us, length us, event | category | flops | bytes accessed | tf_op | source)
XLA Modules:
  0.0 81.7 jit_solution(5975882051747256467)
XLA Ops:
  0.7 0.7 compare_select_fusion
  1.4 0.7 copy.15
  2.1 0.9 %multiply_multiply_fusion.6 = (f32[4,2048]{1,0:T(4,128)}, f32[4,2048]{1,0:T(4,128)}) fusion(f32[2048]{0:T(1024)S(1)} %compare_select_fusion, s32[2048]{0:T(1024)S(1)} %bitcast.6, s32[4]{0:T(128)S(1)} %add_multiply_fusion.3), kind=kLoop, calls=%fused_computation.83 | loop fusion | flops 712704 | bytes 81936 | tf_op jit(solution)/shard_map/mul | solution.py:245
  3.0 0.9 %add_convert_fusion = f32[2,8192]{1,0:T(2,128)S(1)} fusion(s32[2,8192]{1,0:T(2,128)} %param.11), kind=kLoop, calls=%fused_computation.62 | loop fusion | flops 49152 | bytes 131072 | tf_op jit(solution)/shard_map/convert_element_type | solution.py:246
  3.9 0.6 constant_dynamic-slice_fusion.1.sign_ref
  4.5 1.6 %multiply_multiply_fusion.2 = (f32[32,2048]{1,0:T(8,128)}, f32[32,2048]{1,0:T(8,128)}) fusion(f32[2048]{0:T(1024)S(1)} %compare_select_fusion, s32[2048]{0:T(1024)S(1)} %bitcast.7, s32[32]{0:T(128)S(1)} %add_multiply_fusion.4), kind=kLoop, calls=%fused_computation.51 | loop fusion | flops 5701632 | bytes 540800 | tf_op jit(solution)/shard_map/mul | solution.py:242
  6.1 1.0 %broadcast_in_dim.41.back_sign_ref = f32[2,512,128]{2,1,0:T(8,128)} broadcast(f32[2,512]{1,0:T(2,128)S(1)} %constant_dynamic-slice_fusion), dimensions={0,1} | broadcast | bytes 528384 | tf_op jit(solution)/shard_map/broadcast_in_dim | solution.py:250
  7.1 4.0 %select_multiply_fusion = (f32[128,2048]{1,0:T(8,128)}, f32[128,2048]{1,0:T(8,128)}) fusion(s32[2048]{0:T(1024)S(1)} %bitcast.8, s32[128]{0:T(128)S(1)} %multiply_add_fusion.3), kind=kLoop, calls=%fused_computation.20 | loop fusion | flops 22282240 | bytes 2105856 | tf_op jit(solution)/shard_map/mul | solution.py:26
  11.1 63.7 %shard_map.102 = (bf16[128,4096]{1,0:T(8,128)(2,1)}, f32[2,64,128]{2,1,0:T(8,128)}, f32[2,64,128]{2,1,0:T(8,128)}, bf16[2,512,128]{2,1,0:T(8,128)(2,1)}) custom-call(bf16[128,4096]{1,0:T(8,128)(2,1)} %tok_ref.1, bf16[2,8192,128]{2,1,0:T(8,128)(2,1)} %w_ref.1, bf16[2,128,128]{2,1,0:T(8,128)(2,1)} %hc_ref.1, f32[2,4096]{1,0:T(2,128)} %constant_dynamic-slice_fusion.1.sign_ref, ...), custom_call_target="tpu_custom_call" | custom-call | tf_op jit(solution)/shard_map/pallas_call | solution.py:255
  74.8 2.3 %copy.20 = bf16[128,4096]{1,0:T(8,128)(2,1)} copy(bf16[128,4096]{1,0:T(8,128)(2,1)} %get-tuple-element.14) | data formatting | bytes 2097152
  77.1 1.5 %copy.21 = f32[2,64,128]{2,1,0:T(8,128)} copy(f32[2,64,128]{2,1,0:T(8,128)} %get-tuple-element.15) | data formatting | bytes 131072
  78.6 1.5 %copy.22 = f32[2,64,128]{2,1,0:T(8,128)} copy(f32[2,64,128]{2,1,0:T(8,128)} %get-tuple-element.16) | data formatting | bytes 131072
  80.0 1.7 %copy.23 = bf16[2,512,128]{2,1,0:T(8,128)(2,1)} copy(bf16[2,512,128]{2,1,0:T(8,128)(2,1)} %get-tuple-element.17) | data formatting | bytes 524288
  (4 shorter events, 0.0 us)
where the time goes:
time: 82.1 us; the launch traced here: 81.7 us
  Pallas kernels  63.7 us (78%)
  local copies, waits for them, and re-layouts  9.23 us (11%)
  other arithmetic  8.11 us (10%)
    pallas_call x1, Pallas kernels, shards(): pl.pallas_call(functools.partial(step_kernel, low_rows, chunk, token_coun...  63.7 us
    unnamed x5, local copies, waits for them, and re-layouts  7.6 us
    mul x1, other arithmetic, trig(): sine = jnp.where(odd, c, s) * jnp.where(quarter >= 2, -1.0, 1.0)  4.03 us

commit v1 on v0

v1 whole, which is shorter than its diff:
```python
import functools
import math

import jax
import jax.numpy as jnp
from jax import lax
from jax.experimental import pallas as pl
from jax.experimental.pallas import tpu as pltpu
from jax.sharding import PartitionSpec as P

first_fix = 1.0 - 0.9**10
second_fix = 1.0 - 0.95**10
epsilon = 1e-08
bf16, f32 = jnp.bfloat16, jnp.float32
PIECES = 4


def wrap(value, period):
    return value & (period - 1) if period & (period - 1) == 0 else lax.rem(value, period)


def trig(phase, width):
    phase = wrap(phase, 4 * width)
    shift = width.bit_length() - 1
    quarter = (phase + width // 2) >> shift if 1 << shift == width else lax.div(phase + width // 2, width)
    x = (phase - quarter * width).astype(f32) * (math.pi / (2 * width))
    y = x * x
    c = 1.0 + y * (-0.5 + y * (1 / 24 + y * (-1 / 720 + y * (1 / 40320 - y * (1 / 3628800)))))
    s = x * (1.0 + y * (-1 / 6 + y * (1 / 120 + y * (-1 / 5040 + y * (1 / 362880)))))
    quarter = quarter & 3
    odd = (quarter & 1) == 1
    cosine = jnp.where(odd, s, c) * jnp.where((quarter == 1) | (quarter == 2), -1.0, 1.0)
    sine = jnp.where(odd, c, s) * jnp.where(quarter >= 2, -1.0, 1.0)
    return cosine, sine


def dot_last(a, b):
    return lax.dot_general(a, b, (((1,), (1,)), ((), ())), preferred_element_type=f32)


def main_kernel(
    plan,
    tok_ref, w_ref, hc_ref, freq_ref, sign_ref, first_ref, second_ref,
    ig_ref, nf_ref, ns_ref, full_ref,
    tok_all, tok_s, freq, sgn, sgn_b, cb, sb, ca, sa, ra, rb, buf, back, sgn_col,
    hc_all, heads, pair_heads, quad_send, quad_recv, z_send, z_recv, mom, res, res_in, dirs, facc,
    f_send, f_recv, w_own, wp, g_acc, g_send, g_recv,
    loc, core_sems, hx_sems, hf_sems, wx_sems, wy_sems, quad_sems, z_sems, ag_sems,
):
    n_t, nz, nb, low_rows, token_count, width = plan
    rows, lw = tok_all.shape[1], tok_all.shape[2]
    rank = freq.shape[1]
    cr, cols = dirs.shape[1], dirs.shape[2]
    own = cr // 2
    zr = nb * cr
    own_rows = f_send.shape[0]
    half = lw // 2
    part = half // nb
    piece = part // PIECES
    wide = min(512, half)
    me_t, me_d = lax.axis_index("tensor"), lax.axis_index("dp")
    c, q = me_d % 2, me_d // 2
    y, z = q % nb, q // nb
    oc = 1 - c

    def dev(t, zz, yy, cc):
        return {"tensor": t, "dp": (zz * nb + yy) * 2 + cc}

    other = dev(me_t, z, y, oc)

    def xor(a, b):
        total, bit = 0, 1
        while bit < nz:
            total = total + bit * ((a // bit + b // bit) % 2)
            bit *= 2
        return total

    def remote(src, dst, send, recv, device):
        return pltpu.make_async_remote_copy(
            src_ref=src, dst_ref=dst, send_sem=send, recv_sem=recv,
            device_id=device, device_id_type=pl.DeviceIdType.MESH,
        )

    loads = [
        (freq_ref, freq),
        (tok_ref, tok_all.at[c]),
        (sign_ref.at[:, pl.ds(pl.multiple_of(me_t * lw, 128), lw)], sgn),
        (hc_ref, hc_all.at[me_t, c]),
        (sign_ref.at[:, pl.ds(pl.multiple_of(q * 2 * own_rows, 128), 2 * own_rows)], sgn_b),
        (first_ref.at[c], mom.at[0, c]),
        (second_ref.at[c], mom.at[1, c]),
        (w_ref.at[:, pl.ds(pl.multiple_of(me_t * lw + c * half, 128), half), :], w_own),
    ]
    loads = [pltpu.make_async_copy(a, b, loc.at[i]) for i, (a, b) in enumerate(loads)]
    for copy in loads:
        copy.start()

    barrier = pltpu.get_barrier_semaphore()
    peers = [other]
    for dt in range(n_t):
        for dy in range(nb):
            if dt or dy:
                peers.append(dev((me_t + dt) % n_t, z, (y + dy) % nb, c))
    for s in range(1, nz):
        peers.append(dev(me_t, xor(z, s), y, c))
    for device in peers:
        pl.semaphore_signal(barrier, inc=1, device_id=device, device_id_type=pl.DeviceIdType.MESH)

    loads[0].wait()
    f = jnp.where(c == 0, freq[0:1, :], freq[1:2, :])
    scale = jnp.where(f == 0, math.sqrt(1.0 / width), math.sqrt(2.0 / width)).astype(f32)

    def fill(cos_ref, sin_ref, start, stride, scaled):
        def block(r, carry):
            index = r * 8 + lax.broadcasted_iota(jnp.int32, (8, rank), 0)
            cosine, sine = trig((start + stride * index) * f, width)
            if scaled:
                cosine, sine = cosine * scale, sine * scale
            place = pl.ds(pl.multiple_of(r * 8, 8), 8)
            for k in range(nz):
                cos_ref[k, place, :] = cosine[:, k * zr : (k + 1) * zr]
                sin_ref[k, place, :] = sine[:, k * zr : (k + 1) * zr]
            return carry

        lax.fori_loop(0, cos_ref.shape[1] // 8, block, 0)

    fill(cb, sb, 1, 2, False)
    pl.semaphore_wait(barrier, len(peers))

    early = [
        remote(tok_ref, tok_all.at[c], core_sems.at[0, 0], core_sems.at[1, 0], other),
        remote(hc_ref, hc_all.at[me_t, c], core_sems.at[0, 1], core_sems.at[1, 1], other),
        remote(first_ref.at[oc], mom.at[0, c], core_sems.at[0, 2], core_sems.at[1, 2], other),
        remote(second_ref.at[oc], mom.at[1, c], core_sems.at[0, 3], core_sems.at[1, 3], other),
    ]

    def tensor_peer(s):
        return dev((me_t + s) % n_t, z, y, c)

    def hx_copy(s):
        return remote(hc_ref, hc_all.at[me_t, c], hx_sems.at[0, s - 1], hx_sems.at[1, s - 1], tensor_peer(s))

    def hf_copy(s):
        slot = hc_all.at[(me_t + n_t - s) % n_t, c]
        return remote(slot, slot, hf_sems.at[0, s - 1], hf_sems.at[1, s - 1], other)

    def wx_copy(s, p):
        row = y * part + p * piece
        at = pl.ds(pl.multiple_of(((me_t + s) % n_t) * lw + c * half + row, 16), piece)
        to = pl.ds(pl.multiple_of(row, 16), piece)
        return remote(
            w_ref.at[:, at, :], wp.at[s - 1, :, to, :],
            wx_sems.at[0, s - 1, p], wx_sems.at[1, s - 1, p], tensor_peer(s),
        )

    def wy_copy(s, p, dy):
        to = pl.ds(pl.multiple_of(y * part + p * piece, 16), piece)
        slot = wp.at[s - 1, :, to, :]
        return remote(
            slot, slot, wy_sems.at[0, s - 1, p, dy - 1], wy_sems.at[1, s - 1, p, dy - 1],
            dev(me_t, z, (y + dy) % nb, c),
        )

    early[0].start()
    for s in range(1, n_t):
        hx_copy(s).start()
    for copy in early[1:]:
        copy.start()
    for p in range(PIECES):
        for s in range(1, n_t):
            wx_copy(s, p).start()

    fill(ca, sa, 2 * me_t * lw, 2 * low_rows, True)
    fill(ra, rb, 2 * q * 2 * own_rows, 2 * low_rows, True)

    def sign_tokens(k):
        step = min(512, lw)

        def tile(j, carry):
            place = pl.ds(pl.multiple_of(j * step, step), step)
            row = jnp.where(c == 0, sgn[0:1, place], sgn[1:2, place])
            row = (2 * row - 1).astype(f32).astype(bf16)
            tok_s[pl.ds(k, 1), :, place] = tok_all[pl.ds(k, 1), :, place] * row
            return carry

        lax.fori_loop(0, lw // step, tile, 0)

    loads[1].wait()
    loads[2].wait()
    sign_tokens(c)
    for s in range(1, n_t):
        hx_copy(s).wait_recv()
        hf_copy(s).start()
    early[0].wait_recv()
    sign_tokens(oc)

    def tables(a_ref, b_ref, h, k):
        row = pl.ds(h, 1)
        return (a_ref[k, row, :] * cb[k] - b_ref[k, row, :] * sb[k]).astype(bf16)

    def quad_copy(i, dt, dy):
        slot = dt * nb + dy - 1
        t, yy = (me_t + dt) % n_t, (y + dy) % nb
        return remote(
            quad_send.at[i, t, yy], quad_recv.at[i, slot],
            quad_sems.at[0, i, slot], quad_sems.at[1, i, slot], dev(t, z, yy, c),
        )

    quad_slots = [(dt, dy) for dt in range(n_t) for dy in range(nb) if dt or dy]

    def z_copy(i):
        return remote(
            z_send.at[i], z_recv.at[i], z_sems.at[0, i], z_sems.at[1, i], dev(me_t, xor(z, nz - 1 - i), y, c)
        )

    def reduced(i):
        total = quad_send[i, me_t, y].astype(f32)
        for dt, dy in quad_slots:
            quad_copy(i, dt, dy).wait_recv()
            total = total + quad_recv[i, dt * nb + dy - 1].astype(f32)
        return total

    def pass_on(i):
        z_send[i] = reduced(i).astype(bf16)
        z_copy(i).start()

    def chunk(i, carry):
        k = xor(z, nz - 1 - i)

        def build(h, carry):
            buf[pl.ds(pl.multiple_of(h * low_rows, low_rows), low_rows), :] = tables(ca, sa, h, k)
            return carry

        lax.fori_loop(0, lw // low_rows, build, 0, unroll=2)
        projected = jnp.dot(tok_s[...].reshape(2 * rows, lw), buf[...], preferred_element_type=f32).astype(bf16)

        @pl.when(i == 0)
        def _():
            loads[3].wait()
            early[1].wait_recv()
            for s in range(1, n_t):
                hf_copy(s).wait_recv()
            for t in range(n_t):
                heads[:, t * cols : (t + 1) * cols] = hc_all[t, :, pl.ds(c, 1)].reshape(2 * rows, cols)
                for m in range(2):
                    pair_heads[t, :, m * cols : (m + 1) * cols] = hc_all[t, :, m].reshape(2 * rows, cols)

        low = lax.dot_general(
            projected, heads[...], (((0,), (0,)), ((), ())), preferred_element_type=f32
        ).astype(bf16)
        for t in range(n_t):
            for yy in range(nb):
                quad_send[i, t, yy] = low[yy * cr : (yy + 1) * cr, t * cols : (t + 1) * cols]
        for dt, dy in quad_slots:
            quad_copy(i, dt, dy).start()

        @pl.when(i > 0)
        def _():
            pass_on(i - 1)

        return carry

    lax.fori_loop(0, nz, chunk, 0)

    def back_rows(h, carry):
        place = pl.ds(pl.multiple_of(h * low_rows, low_rows), low_rows)
        for k in range(nz):
            back[k, place, :] = tables(ra, rb, h, k)
        return carry

    lax.fori_loop(0, back.shape[1] // low_rows, back_rows, 0)
    loads[4].wait()
    lane = min(128, 2 * own_rows)
    for b in range(2 * own_rows // lane):
        at = slice(b * lane, (b + 1) * lane)
        row = (2 * jnp.where(c == 0, sgn_b[0:1, at], sgn_b[1:2, at]) - 1).astype(f32)
        sgn_col[b * lane : (b + 1) * lane, :] = jnp.broadcast_to(row, (128, lane)).T
    loads[7].wait()

    def own_gradient(j, carry):
        place = pl.ds(pl.multiple_of(j * wide, wide), wide)
        w = jnp.concatenate([w_own[m, place, :] for m in range(2)], axis=1)
        g_acc[:, place] = dot_last(pair_heads[me_t], w)
        return carry

    lax.fori_loop(0, half // wide, own_gradient, 0)
    for i in (5, 6):
        loads[i].wait()
    for i in (2, 3):
        early[i].wait_recv()

    total = reduced(nz - 1)
    for i in range(nz - 1):
        z_copy(i).wait_recv()
        total = total + z_recv[i].astype(f32)
    gradient = (total / math.sqrt(token_count)).reshape(2, own, cols)
    new_first = 0.9 * mom[0] + 0.1 * gradient
    new_second = 0.95 * mom[1] + 0.05 * gradient * gradient
    direction = new_first / first_fix / (jnp.sqrt(new_second / second_fix) + epsilon)
    dirs[pl.ds(z * nb + y, 1)] = direction.astype(bf16).reshape(1, cr, cols)

    def ag_copy(s, dy):
        if dy == 0:
            slot = dirs.at[z * nb + y]
            return remote(slot, slot, ag_sems.at[0, s, 0], ag_sems.at[1, s, 0], dev(me_t, xor(z, s), y, c))
        slot = dirs.at[xor(z, s) * nb + y]
        return remote(
            slot, slot, ag_sems.at[0, s, dy], ag_sems.at[1, s, dy], dev(me_t, z, (y + dy) % nb, c)
        )

    for s in range(nz - 1, 0, -1):
        ag_copy(s, 0).start()
    for dy in range(1, nb):
        ag_copy(0, dy).start()
    res[0] = new_first
    res[1] = new_second
    res_copies = [
        remote(res.at[k, oc], res_in.at[k], core_sems.at[0, 4 + k], core_sems.at[1, 4 + k], other)
        for k in range(2)
    ]
    for copy in res_copies:
        copy.start()

    def relay(p):
        for s in range(1, n_t):
            wx_copy(s, p).wait_recv()
            for dy in range(1, nb):
                wy_copy(s, p, dy).start()

    for p in range(PIECES):
        relay(p)
    for s in range(1, nz):
        ag_copy(s, 0).wait_recv()
        for dy in range(1, nb):
            ag_copy(s, dy).start()
    facc[...] = jnp.zeros_like(facc)
    for s in range(nz):
        for dy in range(1, nb):
            ag_copy(s, dy).wait_recv()
        zz = xor(z, s)
        block = dirs[pl.ds(zz * nb, nb)].reshape(zr, cols)
        facc[...] += jnp.dot(back[zz], block, preferred_element_type=f32)

    def finished(k):
        place = pl.ds(pl.multiple_of(k * own_rows, own_rows), own_rows)
        value, signs = facc[place, :], sgn_col[place, :]
        return jnp.concatenate(
            [value[:, j : j + 128] * signs for j in range(0, cols, 128)], axis=1
        ).astype(bf16)

    f_send[...] = finished(oc)
    f_copy = remote(f_send, f_recv, core_sems.at[0, 6], core_sems.at[1, 6], other)
    f_copy.start()
    full_ref[pl.ds(c, 1)] = finished(c)[None]

    for p in range(PIECES):
        for s in range(1, n_t):
            for dy in range(1, nb):
                wy_copy(s, p, dy).wait_recv()

    def add_gradient(j, carry):
        place = pl.ds(pl.multiple_of(j * wide, wide), wide)
        value = g_acc[:, place]
        for s in range(1, n_t):
            w = jnp.concatenate([wp[s - 1, m, place, :] for m in range(2)], axis=1)
            value = value + dot_last(pair_heads[(me_t + n_t - s) % n_t], w)
        g_acc[:, place] = value
        g_send[:, place] = g_acc[pl.ds(pl.multiple_of(oc * rows, rows), rows), place].astype(bf16)
        mine = g_acc[pl.ds(pl.multiple_of(c * rows, rows), rows), place].astype(bf16)
        ig_ref[pl.ds(c, 1), :, place] = mine[None]
        return carry

    lax.fori_loop(0, half // wide, add_gradient, 0)
    g_copy = remote(g_send, g_recv, core_sems.at[0, 7], core_sems.at[1, 7], other)
    g_copy.start()

    nf_ref[pl.ds(c, 1)] = res[0, pl.ds(c, 1)]
    ns_ref[pl.ds(c, 1)] = res[1, pl.ds(c, 1)]
    for copy in res_copies:
        copy.wait_recv()
    nf_ref[pl.ds(oc, 1)] = res_in[0][None]
    ns_ref[pl.ds(oc, 1)] = res_in[1][None]
    f_copy.wait_recv()
    full_ref[pl.ds(oc, 1)] = f_recv[...][None]
    g_copy.wait_recv()
    ig_ref[pl.ds(oc, 1)] = g_recv[...][None]

    for copy in early + res_copies + [f_copy, g_copy]:
        copy.wait_send()
    for s in range(1, n_t):
        hx_copy(s).wait_send()
        hf_copy(s).wait_send()
        for p in range(PIECES):
            wx_copy(s, p).wait_send()
            for dy in range(1, nb):
                wy_copy(s, p, dy).wait_send()

    def sent(i, carry):
        for dt, dy in quad_slots:
            quad_copy(i, dt, dy).wait_send()
        return carry

    lax.fori_loop(0, nz, sent, 0)
    for i in range(nz - 1):
        z_copy(i).wait_send()
    for s in range(nz):
        for dy in range(nb):
            if s or dy:
                ag_copy(s, dy).wait_send()


def write_kernel(ig, nf, ns, full, ig_out, nf_out, ns_out, full_out, sems):
    half = ig.shape[2]
    copies = [(ig.at[k], ig_out.at[:, k * half : (k + 1) * half]) for k in range(2)]
    copies += [(full, full_out), (nf, nf_out), (ns, ns_out)]
    copies = [pltpu.make_async_copy(a, b, sems.at[i]) for i, (a, b) in enumerate(copies)]
    for copy in copies:
        copy.start()
    for copy in copies:
        copy.wait()


def shards(
    tokens, projection_weights, head_cotangent, frequencies, sign_bits, first_moment, second_moment
):
    rows, lw = tokens.shape
    n_t, n_dp = lax.axis_size("tensor"), lax.axis_size("dp")
    width = lw * n_t
    rank = frequencies.shape[1]
    own, cols = first_moment.shape[1], first_moment.shape[2]
    own_rows = projection_weights.shape[1] // n_dp
    chips = n_dp // 2
    cr = 2 * own
    nb = 2
    while nb * cr % 128:
        nb *= 2
    nz = chips // nb
    zr = nb * cr
    low_rows = min(128, 2 * own_rows)
    up8 = lambda n: -(-n // 8) * 8
    half = lw // 2
    group = n_t * nb - 1

    anywhere, vmem = pl.BlockSpec(memory_space=pltpu.HBM), pl.BlockSpec(memory_space=pltpu.VMEM)
    dma = pltpu.SemaphoreType.DMA
    V = pltpu.VMEM
    plan = (n_t, nz, nb, low_rows, rows * n_dp, width)
    ig, nf, ns, full = pl.pallas_call(
        functools.partial(main_kernel, plan),
        out_shape=(
            jax.ShapeDtypeStruct((2, rows, half), bf16),
            jax.ShapeDtypeStruct((2, own, cols), f32),
            jax.ShapeDtypeStruct((2, own, cols), f32),
            jax.ShapeDtypeStruct((2, own_rows, cols), bf16),
        ),
        in_specs=[anywhere] * 7,
        out_specs=(vmem,) * 4,
        scratch_shapes=[
            V((2, rows, lw), bf16), V((2, rows, lw), bf16), V((2, rank), jnp.int32),
            V((2, lw), jnp.int32), V((2, 2 * own_rows), jnp.int32),
            V((nz, low_rows, zr), f32), V((nz, low_rows, zr), f32),
            V((nz, up8(lw // low_rows), zr), f32), V((nz, up8(lw // low_rows), zr), f32),
            V((nz, up8(2 * own_rows // low_rows), zr), f32), V((nz, up8(2 * own_rows // low_rows), zr), f32),
            V((lw, zr), bf16), V((nz, 2 * own_rows, zr), bf16), V((2 * own_rows, 128), f32),
            V((n_t, 2, 2, rows, cols), bf16), V((2 * rows, n_t * cols), bf16), V((n_t, 2 * rows, 2 * cols), bf16),
            V((nz, n_t, nb, cr, cols), bf16), V((nz, group, cr, cols), bf16),
            V((nz, cr, cols), bf16), V((nz, cr, cols), bf16),
            V((2, 2, own, cols), f32), V((2, 2, own, cols), f32), V((2, own, cols), f32),
            V((nz * nb, cr, cols), bf16), V((2 * own_rows, cols), f32),
            V((own_rows, cols), bf16), V((own_rows, cols), bf16),
            V((2, half, cols), bf16), V((n_t - 1, 2, half, cols), bf16),
            V((2 * rows, half), f32), V((rows, half), bf16), V((rows, half), bf16),
            dma((8,)), dma((2, 8)), dma((2, n_t - 1)), dma((2, n_t - 1)),
            dma((2, n_t - 1, PIECES)), dma((2, n_t - 1, PIECES, nb - 1)),
            dma((2, nz, group)), dma((2, nz)), dma((2, nz, nb)),
        ],
        compiler_params=pltpu.CompilerParams(
            collective_id=0, has_side_effects=True, vmem_limit_bytes=48 * 1024 * 1024
        ),
    )(tokens, projection_weights, head_cotangent, frequencies, sign_bits, first_moment, second_moment)
    return pl.pallas_call(
        write_kernel,
        out_shape=(
            jax.ShapeDtypeStruct((rows, lw), bf16),
            jax.ShapeDtypeStruct((2, own, cols), f32),
            jax.ShapeDtypeStruct((2, own, cols), f32),
            jax.ShapeDtypeStruct((2, own_rows, cols), bf16),
        ),
        in_specs=[vmem] * 4,
        out_specs=(anywhere,) * 4,
        scratch_shapes=[dma((5,))],
        compiler_params=pltpu.CompilerParams(vmem_limit_bytes=8 * 1024 * 1024),
    )(ig, nf, ns, full)


def solution(mesh):
    in_specs = (
        P("dp", "tensor"),
        P(None, None, "tensor"),
        P(None, "dp", "tensor"),
        P(),
        P(),
        P(None, "dp", "tensor"),
        P(None, "dp", "tensor"),
    )
    out_specs = (
        P("dp", "tensor"),
        P(None, "dp", "tensor"),
        P(None, "dp", "tensor"),
        P(None, "dp", "tensor"),
    )
    return jax.shard_map(shards, mesh=mesh, in_specs=in_specs, out_specs=out_specs, check_vma=False)
```

time: 82.1 us -> 54.6 us (0.67)
  the two profiles are of different devices: /device:TPU:21 before, /device:TPU:0 now
where the time goes in v1:
time: 54.6 us; the launch traced here: 54.3 us
  Pallas kernels  48.3 us (88%)
  local copies, waits for them, and re-layouts  5.27 us (10%)
  between operations  0.65 us (1%)
    pallas_call x1, Pallas kernels, shards(): pl.pallas_call(functools.partial(main_kernel, plan), out_shape=(jax.Shape...  47.2 us
    unnamed x12, local copies, waits for them, and re-layouts  5.27 us
    pallas_call x1, Pallas kernels, shards(): pl.pallas_call(write_kernel, out_shape=(jax.ShapeDtypeStruct((rows, lw),...  1.13 us

profile of v1, /device:TPU:0, one launch (start us, length us, event | category | flops | bytes accessed | tf_op | source)
XLA Modules:
  0.0 54.3 jit_solution(15002285735264109636)
XLA Ops:
  0.6 0.0 copy-start
  0.6 1.2 %copy-done = bf16[128,4096]{1,0:T(8,128)(2,1)S(1)} copy-done((bf16[128,4096]{1,0:T(8,128)(2,1)S(1)}, bf16[128,4096]{1,0:T(8,128)(2,1)}, u32[]{:S(2)}) %copy-start) | copy-done | bytes 1048600
  1.9 0.0 copy-start.1
  1.9 0.8 %copy-done.1 = bf16[2,128,128]{2,1,0:T(8,128)(2,1)S(1)} copy-done((bf16[2,128,128]{2,1,0:T(8,128)(2,1)S(1)}, bf16[2,128,128]{2,1,0:T(8,128)(2,1)}, u32[]{:S(2)}) %copy-start.1) | copy-done | bytes 65560
  2.7 0.0 copy-start.2
  2.7 0.8 %copy-done.2 = s32[2,8192]{1,0:T(2,128)S(1)} copy-done((s32[2,8192]{1,0:T(2,128)S(1)}, s32[2,8192]{1,0:T(2,128)}, u32[]{:S(2)}) %copy-start.2) | copy-done | bytes 65560
  3.5 0.0 copy-start.3
  3.5 0.8 %copy-done.3 = f32[2,64,128]{2,1,0:T(8,128)S(1)} copy-done((f32[2,64,128]{2,1,0:T(8,128)S(1)}, f32[2,64,128]{2,1,0:T(8,128)}, u32[]{:S(2)}) %copy-start.3) | copy-done | bytes 65560
  4.4 0.0 copy-start.4
  4.4 0.8 %copy-done.4 = f32[2,64,128]{2,1,0:T(8,128)S(1)} copy-done((f32[2,64,128]{2,1,0:T(8,128)S(1)}, f32[2,64,128]{2,1,0:T(8,128)}, u32[]{:S(2)}) %copy-start.4) | copy-done | bytes 65560
  5.2 0.0 copy-start.5
  5.2 0.7 %copy-done.5 = s32[2,1024]{1,0:T(2,128)S(1)} copy-done((s32[2,1024]{1,0:T(2,128)S(1)}, s32[2,1024]{1,0:T(2,128)}, u32[]{:S(2)}) %copy-start.5) | copy-done | bytes 8216
  5.9 47.2 %shard_map.102 = (bf16[2,128,2048]{2,1,0:T(8,128)(2,1)S(1)}, f32[2,64,128]{2,1,0:T(8,128)S(1)}, f32[2,64,128]{2,1,0:T(8,128)S(1)}, bf16[2,512,128]{2,1,0:T(8,128)(2,1)S(1)}) custom-call(bf16[128,4096]{1,0:T(8,128)(2,1)S(1)} %copy-done, bf16[2,8192,128]{2,1,0:T(8,128)(2,1)} %w_ref.1, bf16[2,128,128]{2,1,0:T(8,128)(2,1)S(1)} %copy-done.1, ...), custom_call_target="tpu_custom_call" | custom-call | tf_op jit(solution)/shard_map/pallas_call | solution.py:448
  53.1 1.1 %shard_map.103 = (bf16[128,4096]{1,0:T(8,128)(2,1)}, f32[2,64,128]{2,1,0:T(8,128)}, f32[2,64,128]{2,1,0:T(8,128)}, bf16[2,512,128]{2,1,0:T(8,128)(2,1)}) custom-call(bf16[2,128,2048]{2,1,0:T(8,128)(2,1)S(1)} %get-tuple-element.8.ig, f32[2,64,128]{2,1,0:T(8,128)S(1)} %get-tuple-element.9.nf, f32[2,64,128]{2,1,0:T(8,128)S(1)} %get-tuple-element.10.ns, ...), custom_call_target="tpu_custom_call" | custom-call | tf_op jit(solution)/shard_map/pallas_call | solution.py:481
Async XLA Ops:
  0.6 1.2 %copy-start = (bf16[128,4096]{1,0:T(8,128)(2,1)S(1)}, bf16[128,4096]{1,0:T(8,128)(2,1)}, u32[]{:S(2)}) copy-start(bf16[128,4096]{1,0:T(8,128)(2,1)} %tok_ref.1) | copy-start | bytes 3145732
  1.9 0.8 %copy-start.1 = (bf16[2,128,128]{2,1,0:T(8,128)(2,1)S(1)}, bf16[2,128,128]{2,1,0:T(8,128)(2,1)}, u32[]{:S(2)}) copy-start(bf16[2,128,128]{2,1,0:T(8,128)(2,1)} %hc_ref.1) | copy-start | bytes 196612
  2.7 0.8 %copy-start.2 = (s32[2,8192]{1,0:T(2,128)S(1)}, s32[2,8192]{1,0:T(2,128)}, u32[]{:S(2)}) copy-start(s32[2,8192]{1,0:T(2,128)} %sign_ref.1) | copy-start | bytes 196612
  3.5 0.8 %copy-start.3 = (f32[2,64,128]{2,1,0:T(8,128)S(1)}, f32[2,64,128]{2,1,0:T(8,128)}, u32[]{:S(2)}) copy-start(f32[2,64,128]{2,1,0:T(8,128)} %first_ref.1) | copy-start | bytes 196612
  4.4 0.8 %copy-start.4 = (f32[2,64,128]{2,1,0:T(8,128)S(1)}, f32[2,64,128]{2,1,0:T(8,128)}, u32[]{:S(2)}) copy-start(f32[2,64,128]{2,1,0:T(8,128)} %second_ref.1) | copy-start | bytes 196612
  5.2 0.7 %copy-start.5 = (s32[2,1024]{1,0:T(2,128)S(1)}, s32[2,1024]{1,0:T(2,128)}, u32[]{:S(2)}) copy-start(s32[2,1024]{1,0:T(2,128)} %freq_ref.1) | copy-start | bytes 24580

commit v2 on v1

--- a/solution.py
+++ b/solution.py
@@ -12,7 +12,7 @@
 second_fix = 1.0 - 0.95**10
 epsilon = 1e-08
 bf16, f32 = jnp.bfloat16, jnp.float32
-PIECES = 4
+RELAY0 = 2
 
 
 def wrap(value, period):
@@ -45,7 +45,7 @@
     tok_all, tok_s, freq, sgn, sgn_b, cb, sb, ca, sa, ra, rb, buf, back, sgn_col,
     hc_all, heads, pair_heads, quad_send, quad_recv, z_send, z_recv, mom, res, res_in, dirs, facc,
     f_send, f_recv, w_own, wp, g_acc, g_send, g_recv,
-    loc, core_sems, hx_sems, hf_sems, wx_sems, wy_sems, quad_sems, z_sems, ag_sems,
+    loc, core_sems, hx_sems, hf_sems, wx_sems, wy_sems, wz_sems, quad_sems, z_sems, ag_sems,
 ):
     n_t, nz, nb, low_rows, token_count, width = plan
     rows, lw = tok_all.shape[1], tok_all.shape[2]
@@ -55,8 +55,8 @@
     zr = nb * cr
     own_rows = f_send.shape[0]
     half = lw // 2
-    part = half // nb
-    piece = part // PIECES
+    part = half // (2 * nb)
+    piece = part // 2
     wide = min(512, half)
     me_t, me_d = lax.axis_index("tensor"), lax.axis_index("dp")
     c, q = me_d % 2, me_d // 2
@@ -106,6 +106,80 @@
     for device in peers:
         pl.semaphore_signal(barrier, inc=1, device_id=device, device_id_type=pl.DeviceIdType.MESH)
 
+    pl.semaphore_wait(barrier, len(peers))
+
+    early = [
+        remote(tok_ref, tok_all.at[c], core_sems.at[0, 0], core_sems.at[1, 0], other),
+        remote(hc_ref, hc_all.at[me_t, c], core_sems.at[0, 1], core_sems.at[1, 1], other),
+        remote(first_ref.at[oc], mom.at[0, c], core_sems.at[0, 2], core_sems.at[1, 2], other),
+        remote(second_ref.at[oc], mom.at[1, c], core_sems.at[0, 3], core_sems.at[1, 3], other),
+    ]
+
+    def tensor_peer(s):
+        return dev((me_t + s) % n_t, z, y, c)
+
+    def hx_copy(s):
+        return remote(hc_ref, hc_all.at[me_t, c], hx_sems.at[0, s - 1], hx_sems.at[1, s - 1], tensor_peer(s))
+
+    def hf_copy(s):
+        slot = hc_all.at[(me_t + n_t - s) % n_t, c]
+        return remote(slot, slot, hf_sems.at[0, s - 1], hf_sems.at[1, s - 1], other)
+
+    def rows_of(yy, zl, p):
+        return pl.multiple_of((yy * 2 + zl) * part + p * piece, 16)
+
+    zl = z % 2
+
+    def wx_copy(s, k):
+        yy, zz, p = (y, zl, k) if k < 2 else ((y + k - 1) % nb, 1 - zl, 1)
+        row = rows_of(yy, zz, p)
+        at = pl.ds(pl.multiple_of(((me_t + s) % n_t) * lw + c * half + row, 16), piece)
+        return remote(
+            w_ref.at[:, at, :], wp.at[s - 1, :, pl.ds(row, piece), :],
+            wx_sems.at[0, s - 1, k], wx_sems.at[1, s - 1, k], tensor_peer(s),
+        )
+
+    def wy_copy(s, p, dy):
+        slot = wp.at[s - 1, :, pl.ds(rows_of(y, zl, p), piece), :]
+        return remote(
+            slot, slot, wy_sems.at[0, s - 1, p, dy - 1], wy_sems.at[1, s - 1, p, dy - 1],
+            dev(me_t, z, (y + dy) % nb, c),
+        )
+
+    def wz_copy(s, k):
+        yy, p = (y, k) if k < 2 else ((y + nb - (k - 1)) % nb, 0)
+        slot = wp.at[s - 1, :, pl.ds(rows_of(yy, zl, p), piece), :]
+        return remote(
+            slot, slot, wz_sems.at[0, s - 1, k], wz_sems.at[1, s - 1, k], dev(me_t, xor(z, 1), y, c)
+        )
+
+    tensor_peers, y_peers = range(1, n_t), range(1, nb)
+
+    def fetch(k):
+        for s in tensor_peers:
+            wx_copy(s, k).start()
+
+    def relay(p):
+        for s in tensor_peers:
+            wx_copy(s, p).wait_recv()
+            for dy in y_peers:
+                wy_copy(s, p, dy).start()
+            wz_copy(s, p).start()
+
+    def forward():
+        for s in tensor_peers:
+            for dy in y_peers:
+                wy_copy(s, 0, dy).wait_recv()
+                wz_copy(s, 1 + dy).start()
+
+    early[0].start()
+    for s in range(1, n_t):
+        hx_copy(s).start()
+    for copy in early[1:]:
+        copy.start()
+    fetch(0)
+    fetch(1)
+
     loads[0].wait()
     f = jnp.where(c == 0, freq[0:1, :], freq[1:2, :])
     scale = jnp.where(f == 0, math.sqrt(1.0 / width), math.sqrt(2.0 / width)).astype(f32)
@@ -125,51 +199,6 @@
         lax.fori_loop(0, cos_ref.shape[1] // 8, block, 0)
 
     fill(cb, sb, 1, 2, False)
-    pl.semaphore_wait(barrier, len(peers))
-
-    early = [
-        remote(tok_ref, tok_all.at[c], core_sems.at[0, 0], core_sems.at[1, 0], other),
-        remote(hc_ref, hc_all.at[me_t, c], core_sems.at[0, 1], core_sems.at[1, 1], other),
-        remote(first_ref.at[oc], mom.at[0, c], core_sems.at[0, 2], core_sems.at[1, 2], other),
-        remote(second_ref.at[oc], mom.at[1, c], core_sems.at[0, 3], core_sems.at[1, 3], other),
-    ]
-
-    def tensor_peer(s):
-        return dev((me_t + s) % n_t, z, y, c)
-
-    def hx_copy(s):
-        return remote(hc_ref, hc_all.at[me_t, c], hx_sems.at[0, s - 1], hx_sems.at[1, s - 1], tensor_peer(s))
-
-    def hf_copy(s):
-        slot = hc_all.at[(me_t + n_t - s) % n_t, c]
-        return remote(slot, slot, hf_sems.at[0, s - 1], hf_sems.at[1, s - 1], other)
-
-    def wx_copy(s, p):
-        row = y * part + p * piece
-        at = pl.ds(pl.multiple_of(((me_t + s) % n_t) * lw + c * half + row, 16), piece)
-        to = pl.ds(pl.multiple_of(row, 16), piece)
-        return remote(
-            w_ref.at[:, at, :], wp.at[s - 1, :, to, :],
-            wx_sems.at[0, s - 1, p], wx_sems.at[1, s - 1, p], tensor_peer(s),
-        )
-
-    def wy_copy(s, p, dy):
-        to = pl.ds(pl.multiple_of(y * part + p * piece, 16), piece)
-        slot = wp.at[s - 1, :, to, :]
-        return remote(
-            slot, slot, wy_sems.at[0, s - 1, p, dy - 1], wy_sems.at[1, s - 1, p, dy - 1],
-            dev(me_t, z, (y + dy) % nb, c),
-        )
-
-    early[0].start()
-    for s in range(1, n_t):
-        hx_copy(s).start()
-    for copy in early[1:]:
-        copy.start()
-    for p in range(PIECES):
-        for s in range(1, n_t):
-            wx_copy(s, p).start()
-
     fill(ca, sa, 2 * me_t * lw, 2 * low_rows, True)
     fill(ra, rb, 2 * q * 2 * own_rows, 2 * low_rows, True)
 
@@ -258,10 +287,16 @@
         def _():
             pass_on(i - 1)
 
+        @pl.when(i == RELAY0)
+        def _():
+            relay(0)
+
         return carry
 
     lax.fori_loop(0, nz, chunk, 0)
 
+    for k in range(2, nb + 1):
+        fetch(k)
     def back_rows(h, carry):
         place = pl.ds(pl.multiple_of(h * low_rows, low_rows), low_rows)
         for k in range(nz):
@@ -284,6 +319,7 @@
         return carry
 
     lax.fori_loop(0, half // wide, own_gradient, 0)
+    relay(1)
     for i in (5, 6):
         loads[i].wait()
     for i in (2, 3):
@@ -321,14 +357,7 @@
     for copy in res_copies:
         copy.start()
 
-    def relay(p):
-        for s in range(1, n_t):
-            wx_copy(s, p).wait_recv()
-            for dy in range(1, nb):
-                wy_copy(s, p, dy).start()
-
-    for p in range(PIECES):
-        relay(p)
+    forward()
     for s in range(1, nz):
         ag_copy(s, 0).wait_recv()
         for dy in range(1, nb):
@@ -353,10 +382,12 @@
     f_copy.start()
     full_ref[pl.ds(c, 1)] = finished(c)[None]
 
-    for p in range(PIECES):
-        for s in range(1, n_t):
-            for dy in range(1, nb):
-                wy_copy(s, p, dy).wait_recv()
+    for s in tensor_peers:
+        for dy in y_peers:
+            wy_copy(s, 1, dy).wait_recv()
+            wx_copy(s, 1 + dy).wait_recv()
+        for k in range(nb + 1):
+            wz_copy(s, k).wait_recv()
 
     def add_gradient(j, carry):
         place = pl.ds(pl.multiple_of(j * wide, wide), wide)
@@ -390,9 +421,11 @@
     for s in range(1, n_t):
         hx_copy(s).wait_send()
         hf_copy(s).wait_send()
-        for p in range(PIECES):
-            wx_copy(s, p).wait_send()
-            for dy in range(1, nb):
+        for k in range(nb + 1):
+            wx_copy(s, k).wait_send()
+            wz_copy(s, k).wait_send()
+        for dy in y_peers:
+            for p in range(2):
                 wy_copy(s, p, dy).wait_send()
 
     def sent(i, carry):
@@ -444,6 +477,7 @@
     anywhere, vmem = pl.BlockSpec(memory_space=pltpu.HBM), pl.BlockSpec(memory_space=pltpu.VMEM)
     dma = pltpu.SemaphoreType.DMA
     V = pltpu.VMEM
+    args = (tokens, projection_weights, head_cotangent, frequencies, sign_bits, first_moment, second_moment)
     plan = (n_t, nz, nb, low_rows, rows * n_dp, width)
     ig, nf, ns, full = pl.pallas_call(
         functools.partial(main_kernel, plan),
@@ -471,13 +505,13 @@
             V((2, half, cols), bf16), V((n_t - 1, 2, half, cols), bf16),
             V((2 * rows, half), f32), V((rows, half), bf16), V((rows, half), bf16),
             dma((8,)), dma((2, 8)), dma((2, n_t - 1)), dma((2, n_t - 1)),
-            dma((2, n_t - 1, PIECES)), dma((2, n_t - 1, PIECES, nb - 1)),
+            dma((2, n_t - 1, nb + 1)), dma((2, n_t - 1, 2, nb - 1)), dma((2, n_t - 1, nb + 1)),
             dma((2, nz, group)), dma((2, nz)), dma((2, nz, nb)),
         ],
         compiler_params=pltpu.CompilerParams(
             collective_id=0, has_side_effects=True, vmem_limit_bytes=48 * 1024 * 1024
         ),
-    )(tokens, projection_weights, head_cotangent, frequencies, sign_bits, first_moment, second_moment)
+    )(*(pltpu.with_memory_space_constraint(a, pltpu.HBM) for a in args))
     return pl.pallas_call(
         write_kernel,
         out_shape=(

time: 54.6 us -> 39.5 us (0.72)
  Pallas kernels: 48.3 us -> 38.7 us
  local copies, waits for them, and re-layouts: 5.27 us -> 0 us
    pallas_call x1, Pallas kernels: 47.2 us -> 37.6 us  [shards(): pl.pallas_call(functools.partial(main_kernel, plan), out_shape=(jax.Shape...]
    unnamed x12 -> x0, local copies, waits for them, and re-layouts: 5.27 us -> none
where the time goes in v2:
time: 39.5 us; the launch traced here: 39.3 us
  Pallas kernels  38.7 us (98%)
  between operations  0.64 us (2%)
    pallas_call x1, Pallas kernels, shards(): pl.pallas_call(functools.partial(main_kernel, plan), out_shape=(jax.Shape...  37.6 us
    pallas_call x1, Pallas kernels, shards(): pl.pallas_call(write_kernel, out_shape=(jax.ShapeDtypeStruct((rows, lw),...  1.13 us

profile of v2, /device:TPU:0, one launch (start us, length us, event | category | flops | bytes accessed | tf_op | source)
XLA Modules:
  0.0 39.3 jit_solution(14831808783514947815)
XLA Ops:
  0.6 37.6 %shard_map.102 = (bf16[2,128,2048]{2,1,0:T(8,128)(2,1)S(1)}, f32[2,64,128]{2,1,0:T(8,128)S(1)}, f32[2,64,128]{2,1,0:T(8,128)S(1)}, bf16[2,512,128]{2,1,0:T(8,128)(2,1)S(1)}) custom-call(bf16[128,4096]{1,0:T(8,128)(2,1)} %tok_ref.1, bf16[2,8192,128]{2,1,0:T(8,128)(2,1)} %w_ref.1, bf16[2,128,128]{2,1,0:T(8,128)(2,1)} %hc_ref.1, s32[2,1024]{1,0:T(2,128)} %freq_ref.1, ...), custom_call_target="tpu_custom_call" | custom-call | tf_op jit(solution)/shard_map/pallas_call | solution.py:482
  38.2 1.1 %shard_map.103 = (bf16[128,4096]{1,0:T(8,128)(2,1)}, f32[2,64,128]{2,1,0:T(8,128)}, f32[2,64,128]{2,1,0:T(8,128)}, bf16[2,512,128]{2,1,0:T(8,128)(2,1)}) custom-call(bf16[2,128,2048]{2,1,0:T(8,128)(2,1)S(1)} %get-tuple-element.8.ig, f32[2,64,128]{2,1,0:T(8,128)S(1)} %get-tuple-element.9.nf, f32[2,64,128]{2,1,0:T(8,128)S(1)} %get-tuple-element.10.ns, ...), custom_call_target="tpu_custom_call" | custom-call | tf_op jit(solution)/shard_map/pallas_call | solution.py:515

commit v3 on v2

--- a/solution.py
+++ b/solution.py
@@ -42,10 +42,10 @@
     plan,
     tok_ref, w_ref, hc_ref, freq_ref, sign_ref, first_ref, second_ref,
     ig_ref, nf_ref, ns_ref, full_ref,
-    tok_all, tok_s, freq, sgn, sgn_b, cb, sb, ca, sa, ra, rb, buf, back, sgn_col,
+    tok_all, tok_s, freq, sgn, sgn_b, cb, sb, ca, sa, ra, rb, back, sgn_col,
     hc_all, heads, pair_heads, quad_send, quad_recv, z_send, z_recv, mom, res, res_in, dirs, facc,
     f_send, f_recv, w_own, wp, g_acc, g_send, g_recv,
-    loc, core_sems, hx_sems, hf_sems, wx_sems, wy_sems, wz_sems, quad_sems, z_sems, ag_sems,
+    loc, core_sems, tok_sems, hx_sems, hf_sems, wx_sems, wy_sems, wz_sems, quad_sems, z_sems, ag_sems,
 ):
     n_t, nz, nb, low_rows, token_count, width = plan
     rows, lw = tok_all.shape[1], tok_all.shape[2]
@@ -58,6 +58,7 @@
     part = half // (2 * nb)
     piece = part // 2
     wide = min(512, half)
+    deep = min(2048, lw)
     me_t, me_d = lax.axis_index("tensor"), lax.axis_index("dp")
     c, q = me_d % 2, me_d // 2
     y, z = q % nb, q // nb
@@ -101,84 +102,12 @@
         for dy in range(nb):
             if dt or dy:
                 peers.append(dev((me_t + dt) % n_t, z, (y + dy) % nb, c))
+    for dt in range(1, n_t):
+        peers.append(dev((me_t + dt) % n_t, z, y, oc))
     for s in range(1, nz):
         peers.append(dev(me_t, xor(z, s), y, c))
     for device in peers:
         pl.semaphore_signal(barrier, inc=1, device_id=device, device_id_type=pl.DeviceIdType.MESH)
-
-    pl.semaphore_wait(barrier, len(peers))
-
-    early = [
-        remote(tok_ref, tok_all.at[c], core_sems.at[0, 0], core_sems.at[1, 0], other),
-        remote(hc_ref, hc_all.at[me_t, c], core_sems.at[0, 1], core_sems.at[1, 1], other),
-        remote(first_ref.at[oc], mom.at[0, c], core_sems.at[0, 2], core_sems.at[1, 2], other),
-        remote(second_ref.at[oc], mom.at[1, c], core_sems.at[0, 3], core_sems.at[1, 3], other),
-    ]
-
-    def tensor_peer(s):
-        return dev((me_t + s) % n_t, z, y, c)
-
-    def hx_copy(s):
-        return remote(hc_ref, hc_all.at[me_t, c], hx_sems.at[0, s - 1], hx_sems.at[1, s - 1], tensor_peer(s))
-
-    def hf_copy(s):
-        slot = hc_all.at[(me_t + n_t - s) % n_t, c]
-        return remote(slot, slot, hf_sems.at[0, s - 1], hf_sems.at[1, s - 1], other)
-
-    def rows_of(yy, zl, p):
-        return pl.multiple_of((yy * 2 + zl) * part + p * piece, 16)
-
-    zl = z % 2
-
-    def wx_copy(s, k):
-        yy, zz, p = (y, zl, k) if k < 2 else ((y + k - 1) % nb, 1 - zl, 1)
-        row = rows_of(yy, zz, p)
-        at = pl.ds(pl.multiple_of(((me_t + s) % n_t) * lw + c * half + row, 16), piece)
-        return remote(
-            w_ref.at[:, at, :], wp.at[s - 1, :, pl.ds(row, piece), :],
-            wx_sems.at[0, s - 1, k], wx_sems.at[1, s - 1, k], tensor_peer(s),
-        )
-
-    def wy_copy(s, p, dy):
-        slot = wp.at[s - 1, :, pl.ds(rows_of(y, zl, p), piece), :]
-        return remote(
-            slot, slot, wy_sems.at[0, s - 1, p, dy - 1], wy_sems.at[1, s - 1, p, dy - 1],
-            dev(me_t, z, (y + dy) % nb, c),
-        )
-
-    def wz_copy(s, k):
-        yy, p = (y, k) if k < 2 else ((y + nb - (k - 1)) % nb, 0)
-        slot = wp.at[s - 1, :, pl.ds(rows_of(yy, zl, p), piece), :]
-        return remote(
-            slot, slot, wz_sems.at[0, s - 1, k], wz_sems.at[1, s - 1, k], dev(me_t, xor(z, 1), y, c)
-        )
-
-    tensor_peers, y_peers = range(1, n_t), range(1, nb)
-
-    def fetch(k):
-        for s in tensor_peers:
-            wx_copy(s, k).start()
-
-    def relay(p):
-        for s in tensor_peers:
-            wx_copy(s, p).wait_recv()
-            for dy in y_peers:
-                wy_copy(s, p, dy).start()
-            wz_copy(s, p).start()
-
-    def forward():
-        for s in tensor_peers:
-            for dy in y_peers:
-                wy_copy(s, 0, dy).wait_recv()
-                wz_copy(s, 1 + dy).start()
-
-    early[0].start()
-    for s in range(1, n_t):
-        hx_copy(s).start()
-    for copy in early[1:]:
-        copy.start()
-    fetch(0)
-    fetch(1)
 
     loads[0].wait()
     f = jnp.where(c == 0, freq[0:1, :], freq[1:2, :])
@@ -199,29 +128,104 @@
         lax.fori_loop(0, cos_ref.shape[1] // 8, block, 0)
 
     fill(cb, sb, 1, 2, False)
+    pl.semaphore_wait(barrier, len(peers))
+
+    early = [
+        remote(hc_ref, hc_all.at[me_t, c], core_sems.at[0, 0], core_sems.at[1, 0], other),
+        remote(first_ref.at[oc], mom.at[0, c], core_sems.at[0, 1], core_sems.at[1, 1], other),
+        remote(second_ref.at[oc], mom.at[1, c], core_sems.at[0, 2], core_sems.at[1, 2], other),
+    ]
+
+    def tensor_peer(s):
+        return dev((me_t + s) % n_t, z, y, c)
+
+    def hx_copy(s, k):
+        m = (c + k) % 2
+        return remote(
+            hc_ref.at[m], hc_all.at[me_t, c, m], hx_sems.at[0, s - 1, k], hx_sems.at[1, s - 1, k],
+            dev((me_t + s) % n_t, z, y, m),
+        )
+
+    def hf_copy(s):
+        slot = hc_all.at[(me_t + n_t - s) % n_t, :, c]
+        return remote(slot, slot, hf_sems.at[0, s - 1], hf_sems.at[1, s - 1], other)
+
+    def tok_copy(p):
+        place = slice(p * (lw // 4), (p + 1) * (lw // 4))
+        return remote(
+            tok_ref.at[:, place], tok_all.at[c, :, place], tok_sems.at[0, p], tok_sems.at[1, p], other
+        )
+
+    def rows_of(yy, zl, p):
+        return pl.multiple_of((yy * 2 + zl) * part + p * piece, 16)
+
+    zl = z % 2
+
+    def wx_copy(s, k):
+        yy, zz, p = (y, zl, k) if k < 2 else ((y + k - 1) % nb, 1 - zl, 1)
+        row = rows_of(yy, zz, p)
+        at = pl.ds(pl.multiple_of(((me_t + s) % n_t) * lw + c * half + row, 16), piece)
+        return remote(
+            w_ref.at[:, at, :], wp.at[s - 1, :, pl.ds(row, piece), :],
+            wx_sems.at[0, s - 1, k], wx_sems.at[1, s - 1, k], tensor_peer(s),
+        )
+
+    def wy_copy(s, p, dy):
+        slot = wp.at[s - 1, :, pl.ds(rows_of(y, zl, p), piece), :]
+        return remote(
+            slot, slot, wy_sems.at[0, s - 1, p, dy - 1], wy_sems.at[1, s - 1, p, dy - 1],
+            dev(me_t, z, (y + dy) % nb, c),
+        )
+
+    def wz_copy(s, k):
+        yy, p = (y, k) if k < 2 else ((y + nb - (k - 1)) % nb, 0)
+        slot = wp.at[s - 1, :, pl.ds(rows_of(yy, zl, p), piece), :]
+        return remote(
+            slot, slot, wz_sems.at[0, s - 1, k], wz_sems.at[1, s - 1, k], dev(me_t, xor(z, 1), y, c)
+        )
+
+    tensor_peers, y_peers = range(1, n_t), range(1, nb)
+
+    def fetch(k):
+        for s in tensor_peers:
+            wx_copy(s, k).start()
+
+    def relay(p):
+        for s in tensor_peers:
+            wx_copy(s, p).wait_recv()
+            for dy in y_peers:
+                wy_copy(s, p, dy).start()
+            wz_copy(s, p).start()
+
+    def forward():
+        for s in tensor_peers:
+            for dy in y_peers:
+                wy_copy(s, 0, dy).wait_recv()
+                wz_copy(s, 1 + dy).start()
+
+    for s in range(1, n_t):
+        for k in range(2):
+            hx_copy(s, k).start()
+    for p in range(4):
+        tok_copy(p).start()
+    for copy in early:
+        copy.start()
+    fetch(0)
+    fetch(1)
+
     fill(ca, sa, 2 * me_t * lw, 2 * low_rows, True)
-    fill(ra, rb, 2 * q * 2 * own_rows, 2 * low_rows, True)
-
-    def sign_tokens(k):
-        step = min(512, lw)
-
-        def tile(j, carry):
-            place = pl.ds(pl.multiple_of(j * step, step), step)
+
+    def sign_tokens(k, start, count):
+        for j in range(start, start + count, count // 2):
+            place = slice(j, j + count // 2)
             row = jnp.where(c == 0, sgn[0:1, place], sgn[1:2, place])
             row = (2 * row - 1).astype(f32).astype(bf16)
             tok_s[pl.ds(k, 1), :, place] = tok_all[pl.ds(k, 1), :, place] * row
-            return carry
-
-        lax.fori_loop(0, lw // step, tile, 0)
 
     loads[1].wait()
     loads[2].wait()
-    sign_tokens(c)
-    for s in range(1, n_t):
-        hx_copy(s).wait_recv()
-        hf_copy(s).start()
-    early[0].wait_recv()
-    sign_tokens(oc)
+    for p in range(4):
+        sign_tokens(c, p * (lw // 4), lw // 4)
 
     def tables(a_ref, b_ref, h, k):
         row = pl.ds(h, 1)
@@ -253,27 +257,16 @@
         z_send[i] = reduced(i).astype(bf16)
         z_copy(i).start()
 
-    def chunk(i, carry):
-        k = xor(z, nz - 1 - i)
-
-        def build(h, carry):
-            buf[pl.ds(pl.multiple_of(h * low_rows, low_rows), low_rows), :] = tables(ca, sa, h, k)
-            return carry
-
-        lax.fori_loop(0, lw // low_rows, build, 0, unroll=2)
-        projected = jnp.dot(tok_s[...].reshape(2 * rows, lw), buf[...], preferred_element_type=f32).astype(bf16)
-
-        @pl.when(i == 0)
-        def _():
-            loads[3].wait()
-            early[1].wait_recv()
-            for s in range(1, n_t):
-                hf_copy(s).wait_recv()
-            for t in range(n_t):
-                heads[:, t * cols : (t + 1) * cols] = hc_all[t, :, pl.ds(c, 1)].reshape(2 * rows, cols)
-                for m in range(2):
-                    pair_heads[t, :, m * cols : (m + 1) * cols] = hc_all[t, :, m].reshape(2 * rows, cols)
-
+    def project(k, step, ready):
+        projected = 0.0
+        for j in range(0, lw, step):
+            ready(j)
+            basis = jnp.concatenate([tables(ca, sa, (j + h) // low_rows, k) for h in range(0, step, low_rows)], axis=0)
+            signed = tok_s[:, :, j : j + step].reshape(2 * rows, step)
+            projected = projected + jnp.dot(signed, basis, preferred_element_type=f32)
+        return projected.astype(bf16)
+
+    def low_rank(i, projected):
         low = lax.dot_general(
             projected, heads[...], (((0,), (0,)), ((), ())), preferred_element_type=f32
         ).astype(bf16)
@@ -283,20 +276,32 @@
         for dt, dy in quad_slots:
             quad_copy(i, dt, dy).start()
 
-        @pl.when(i > 0)
-        def _():
-            pass_on(i - 1)
-
-        @pl.when(i == RELAY0)
-        def _():
-            relay(0)
-
+    def arrive(j):
+        tok_copy(j // (lw // 4)).wait_recv()
+        sign_tokens(oc, j, lw // 4)
+
+    projected = project(xor(z, nz - 1), lw // 4, arrive)
+    loads[3].wait()
+    early[0].wait_recv()
+    for s in tensor_peers:
+        for k in range(2):
+            hx_copy(s, k).wait_recv()
+    for t in range(n_t):
+        heads[:, t * cols : (t + 1) * cols] = hc_all[t, :, pl.ds(c, 1)].reshape(2 * rows, cols)
+    low_rank(0, projected)
+    for s in tensor_peers:
+        hf_copy(s).start()
+
+    def chunk(i, carry):
+        low_rank(i, project(xor(z, nz - 1 - i), deep, lambda j: None))
         return carry
 
-    lax.fori_loop(0, nz, chunk, 0)
-
-    for k in range(2, nb + 1):
-        fetch(k)
+    lax.fori_loop(1, nz, chunk, 0)
+
+    relay(0)
+    for i in range(nz - 1):
+        pass_on(i)
+    fill(ra, rb, 2 * q * 2 * own_rows, 2 * low_rows, True)
     def back_rows(h, carry):
         place = pl.ds(pl.multiple_of(h * low_rows, low_rows), low_rows)
         for k in range(nz):
@@ -311,6 +316,11 @@
         row = (2 * jnp.where(c == 0, sgn_b[0:1, at], sgn_b[1:2, at]) - 1).astype(f32)
         sgn_col[b * lane : (b + 1) * lane, :] = jnp.broadcast_to(row, (128, lane)).T
     loads[7].wait()
+    for s in tensor_peers:
+        hf_copy(s).wait_recv()
+    for t in range(n_t):
+        for m in range(2):
+            pair_heads[t, :, m * cols : (m + 1) * cols] = hc_all[t, :, m].reshape(2 * rows, cols)
 
     def own_gradient(j, carry):
         place = pl.ds(pl.multiple_of(j * wide, wide), wide)
@@ -322,10 +332,12 @@
     relay(1)
     for i in (5, 6):
         loads[i].wait()
-    for i in (2, 3):
+    for i in (1, 2):
         early[i].wait_recv()
 
     total = reduced(nz - 1)
+    for k in range(2, nb + 1):
+        fetch(k)
     for i in range(nz - 1):
         z_copy(i).wait_recv()
         total = total + z_recv[i].astype(f32)
@@ -351,7 +363,7 @@
     res[0] = new_first
     res[1] = new_second
     res_copies = [
-        remote(res.at[k, oc], res_in.at[k], core_sems.at[0, 4 + k], core_sems.at[1, 4 + k], other)
+        remote(res.at[k, oc], res_in.at[k], core_sems.at[0, 3 + k], core_sems.at[1, 3 + k], other)
         for k in range(2)
     ]
     for copy in res_copies:
@@ -362,26 +374,6 @@
         ag_copy(s, 0).wait_recv()
         for dy in range(1, nb):
             ag_copy(s, dy).start()
-    facc[...] = jnp.zeros_like(facc)
-    for s in range(nz):
-        for dy in range(1, nb):
-            ag_copy(s, dy).wait_recv()
-        zz = xor(z, s)
-        block = dirs[pl.ds(zz * nb, nb)].reshape(zr, cols)
-        facc[...] += jnp.dot(back[zz], block, preferred_element_type=f32)
-
-    def finished(k):
-        place = pl.ds(pl.multiple_of(k * own_rows, own_rows), own_rows)
-        value, signs = facc[place, :], sgn_col[place, :]
-        return jnp.concatenate(
-            [value[:, j : j + 128] * signs for j in range(0, cols, 128)], axis=1
-        ).astype(bf16)
-
-    f_send[...] = finished(oc)
-    f_copy = remote(f_send, f_recv, core_sems.at[0, 6], core_sems.at[1, 6], other)
-    f_copy.start()
-    full_ref[pl.ds(c, 1)] = finished(c)[None]
-
     for s in tensor_peers:
         for dy in y_peers:
             wy_copy(s, 1, dy).wait_recv()
@@ -402,7 +394,7 @@
         return carry
 
     lax.fori_loop(0, half // wide, add_gradient, 0)
-    g_copy = remote(g_send, g_recv, core_sems.at[0, 7], core_sems.at[1, 7], other)
+    g_copy = remote(g_send, g_recv, core_sems.at[0, 6], core_sems.at[1, 6], other)
     g_copy.start()
 
     nf_ref[pl.ds(c, 1)] = res[0, pl.ds(c, 1)]
@@ -411,15 +403,38 @@
         copy.wait_recv()
     nf_ref[pl.ds(oc, 1)] = res_in[0][None]
     ns_ref[pl.ds(oc, 1)] = res_in[1][None]
-    f_copy.wait_recv()
+    facc[...] = jnp.zeros_like(facc)
+    for s in range(nz):
+        for dy in range(1, nb):
+            ag_copy(s, dy).wait_recv()
+        zz = xor(z, s)
+        block = dirs[pl.ds(zz * nb, nb)].reshape(zr, cols)
+        facc[...] += jnp.dot(back[zz], block, preferred_element_type=f32)
+
+    def finished(k):
+        place = pl.ds(pl.multiple_of(k * own_rows, own_rows), own_rows)
+        value, signs = facc[place, :], sgn_col[place, :]
+        return jnp.concatenate(
+            [value[:, j : j + 128] * signs for j in range(0, cols, 128)], axis=1
+        ).astype(bf16)
+
+    f_send[...] = finished(oc)
+    f_copy = remote(f_send, f_recv, core_sems.at[0, 5], core_sems.at[1, 5], other)
+    f_copy.start()
+    full_ref[pl.ds(c, 1)] = finished(c)[None]
+
+    for copy in (g_copy, f_copy):
+        copy.wait_recv()
+    ig_ref[pl.ds(oc, 1)] = g_recv[...][None]
     full_ref[pl.ds(oc, 1)] = f_recv[...][None]
-    g_copy.wait_recv()
-    ig_ref[pl.ds(oc, 1)] = g_recv[...][None]
-
+
+    for p in range(4):
+        tok_copy(p).wait_send()
     for copy in early + res_copies + [f_copy, g_copy]:
         copy.wait_send()
     for s in range(1, n_t):
-        hx_copy(s).wait_send()
+        for k in range(2):
+            hx_copy(s, k).wait_send()
         hf_copy(s).wait_send()
         for k in range(nb + 1):
             wx_copy(s, k).wait_send()
@@ -495,7 +510,7 @@
             V((nz, low_rows, zr), f32), V((nz, low_rows, zr), f32),
             V((nz, up8(lw // low_rows), zr), f32), V((nz, up8(lw // low_rows), zr), f32),
             V((nz, up8(2 * own_rows // low_rows), zr), f32), V((nz, up8(2 * own_rows // low_rows), zr), f32),
-            V((lw, zr), bf16), V((nz, 2 * own_rows, zr), bf16), V((2 * own_rows, 128), f32),
+            V((nz, 2 * own_rows, zr), bf16), V((2 * own_rows, 128), f32),
             V((n_t, 2, 2, rows, cols), bf16), V((2 * rows, n_t * cols), bf16), V((n_t, 2 * rows, 2 * cols), bf16),
             V((nz, n_t, nb, cr, cols), bf16), V((nz, group, cr, cols), bf16),
             V((nz, cr, cols), bf16), V((nz, cr, cols), bf16),
@@ -504,7 +519,7 @@
             V((own_rows, cols), bf16), V((own_rows, cols), bf16),
             V((2, half, cols), bf16), V((n_t - 1, 2, half, cols), bf16),
             V((2 * rows, half), f32), V((rows, half), bf16), V((rows, half), bf16),
-            dma((8,)), dma((2, 8)), dma((2, n_t - 1)), dma((2, n_t - 1)),
+            dma((8,)), dma((2, 7)), dma((2, 4)), dma((2, n_t - 1, 2)), dma((2, n_t - 1)),
             dma((2, n_t - 1, nb + 1)), dma((2, n_t - 1, 2, nb - 1)), dma((2, n_t - 1, nb + 1)),
             dma((2, nz, group)), dma((2, nz)), dma((2, nz, nb)),
         ],

time: 39.5 us -> 36.4 us (0.922)
  Pallas kernels: 38.7 us -> 35.6 us
    pallas_call x1, Pallas kernels: 37.6 us -> 34.5 us  [shards(): pl.pallas_call(functools.partial(main_kernel, plan), out_shape=(jax.Shape...]
where the time goes in v3:
time: 36.4 us; the launch traced here: 36.2 us
  Pallas kernels  35.6 us (98%)
  between operations  0.64 us (2%)
    pallas_call x1, Pallas kernels, shards(): pl.pallas_call(functools.partial(main_kernel, plan), out_shape=(jax.Shape...  34.5 us
    pallas_call x1, Pallas kernels, shards(): pl.pallas_call(write_kernel, out_shape=(jax.ShapeDtypeStruct((rows, lw),...  1.13 us

profile of v3, /device:TPU:0, one launch (start us, length us, event | category | flops | bytes accessed | tf_op | source)
XLA Modules:
  0.0 36.2 jit_solution(10302941018502136976)
XLA Ops:
  0.6 34.5 %shard_map.102 = (bf16[2,128,2048]{2,1,0:T(8,128)(2,1)S(1)}, f32[2,64,128]{2,1,0:T(8,128)S(1)}, f32[2,64,128]{2,1,0:T(8,128)S(1)}, bf16[2,512,128]{2,1,0:T(8,128)(2,1)S(1)}) custom-call(bf16[128,4096]{1,0:T(8,128)(2,1)} %tok_ref.1, bf16[2,8192,128]{2,1,0:T(8,128)(2,1)} %w_ref.1, bf16[2,128,128]{2,1,0:T(8,128)(2,1)} %hc_ref.1, s32[2,1024]{1,0:T(2,128)} %freq_ref.1, ...), custom_call_target="tpu_custom_call" | custom-call | tf_op jit(solution)/shard_map/pallas_call | solution.py:497
  35.1 1.1 %shard_map.103 = (bf16[128,4096]{1,0:T(8,128)(2,1)}, f32[2,64,128]{2,1,0:T(8,128)}, f32[2,64,128]{2,1,0:T(8,128)}, bf16[2,512,128]{2,1,0:T(8,128)(2,1)}) custom-call(bf16[2,128,2048]{2,1,0:T(8,128)(2,1)S(1)} %get-tuple-element.8.ig, f32[2,64,128]{2,1,0:T(8,128)S(1)} %get-tuple-element.9.nf, f32[2,64,128]{2,1,0:T(8,128)S(1)} %get-tuple-element.10.ns, ...), custom_call_target="tpu_custom_call" | custom-call | tf_op jit(solution)/shard_map/pallas_call | solution.py:530

commit v4 on v3

--- a/solution.py
+++ b/solution.py
@@ -43,9 +43,9 @@
     tok_ref, w_ref, hc_ref, freq_ref, sign_ref, first_ref, second_ref,
     ig_ref, nf_ref, ns_ref, full_ref,
     tok_all, tok_s, freq, sgn, sgn_b, cb, sb, ca, sa, ra, rb, back, sgn_col,
-    hc_all, heads, pair_heads, quad_send, quad_recv, z_send, z_recv, mom, res, res_in, dirs, facc,
+    hc_all, heads, pair_heads, y_send, y_recv, x_send, x_recv, z_send, z_recv, mom, res, res_in, dirs, facc,
     f_send, f_recv, w_own, wp, g_acc, g_send, g_recv,
-    loc, core_sems, tok_sems, hx_sems, hf_sems, wx_sems, wy_sems, wz_sems, quad_sems, z_sems, ag_sems,
+    loc, core_sems, tok_sems, hx_sems, hf_sems, wx_sems, wy_sems, wz_sems, y_sems, x_sems, z_sems, ag_sems,
 ):
     n_t, nz, nb, low_rows, token_count, width = plan
     rows, lw = tok_all.shape[1], tok_all.shape[2]
@@ -98,12 +98,10 @@
 
     barrier = pltpu.get_barrier_semaphore()
     peers = [other]
-    for dt in range(n_t):
-        for dy in range(nb):
-            if dt or dy:
-                peers.append(dev((me_t + dt) % n_t, z, (y + dy) % nb, c))
+    for dy in range(1, nb):
+        peers.append(dev(me_t, z, (y + dy) % nb, c))
     for dt in range(1, n_t):
-        peers.append(dev((me_t + dt) % n_t, z, y, oc))
+        peers += [dev((me_t + dt) % n_t, z, y, c), dev((me_t + dt) % n_t, z, y, oc)]
     for s in range(1, nz):
         peers.append(dev(me_t, xor(z, s), y, c))
     for device in peers:
@@ -162,8 +160,8 @@
     zl = z % 2
 
     def wx_copy(s, k):
-        yy, zz, p = (y, zl, k) if k < 2 else ((y + k - 1) % nb, 1 - zl, 1)
-        row = rows_of(yy, zz, p)
+        yy, zz = (y, zl) if k < 2 else ((y + k // 2) % nb, 1 - zl)
+        row = rows_of(yy, zz, k % 2)
         at = pl.ds(pl.multiple_of(((me_t + s) % n_t) * lw + c * half + row, 16), piece)
         return remote(
             w_ref.at[:, at, :], wp.at[s - 1, :, pl.ds(row, piece), :],
@@ -177,11 +175,10 @@
             dev(me_t, z, (y + dy) % nb, c),
         )
 
-    def wz_copy(s, k):
-        yy, p = (y, k) if k < 2 else ((y + nb - (k - 1)) % nb, 0)
-        slot = wp.at[s - 1, :, pl.ds(rows_of(yy, zl, p), piece), :]
-        return remote(
-            slot, slot, wz_sems.at[0, s - 1, k], wz_sems.at[1, s - 1, k], dev(me_t, xor(z, 1), y, c)
+    def wz_copy(s, p):
+        slot = wp.at[s - 1, :, pl.ds(rows_of(y, zl, p), piece), :]
+        return remote(
+            slot, slot, wz_sems.at[0, s - 1, p], wz_sems.at[1, s - 1, p], dev(me_t, xor(z, 1), y, c)
         )
 
     tensor_peers, y_peers = range(1, n_t), range(1, nb)
@@ -190,18 +187,15 @@
         for s in tensor_peers:
             wx_copy(s, k).start()
 
-    def relay(p):
+    def relay_z(p):
         for s in tensor_peers:
             wx_copy(s, p).wait_recv()
+            wz_copy(s, p).start()
+
+    def relay_y(p):
+        for s in tensor_peers:
             for dy in y_peers:
                 wy_copy(s, p, dy).start()
-            wz_copy(s, p).start()
-
-    def forward():
-        for s in tensor_peers:
-            for dy in y_peers:
-                wy_copy(s, 0, dy).wait_recv()
-                wz_copy(s, 1 + dy).start()
 
     for s in range(1, n_t):
         for k in range(2):
@@ -231,31 +225,41 @@
         row = pl.ds(h, 1)
         return (a_ref[k, row, :] * cb[k] - b_ref[k, row, :] * sb[k]).astype(bf16)
 
-    def quad_copy(i, dt, dy):
-        slot = dt * nb + dy - 1
-        t, yy = (me_t + dt) % n_t, (y + dy) % nb
-        return remote(
-            quad_send.at[i, t, yy], quad_recv.at[i, slot],
-            quad_sems.at[0, i, slot], quad_sems.at[1, i, slot], dev(t, z, yy, c),
-        )
-
-    quad_slots = [(dt, dy) for dt in range(n_t) for dy in range(nb) if dt or dy]
+    def y_copy(i, dy):
+        yy = (y + dy) % nb
+        return remote(
+            y_send.at[i, yy], y_recv.at[i, dy - 1], y_sems.at[0, i, dy - 1], y_sems.at[1, i, dy - 1],
+            dev(me_t, z, yy, c),
+        )
+
+    def x_copy(i, s):
+        return remote(
+            x_send.at[i, (me_t + s) % n_t], x_recv.at[i, s - 1],
+            x_sems.at[0, i, s - 1], x_sems.at[1, i, s - 1], tensor_peer(s),
+        )
 
     def z_copy(i):
         return remote(
             z_send.at[i], z_recv.at[i], z_sems.at[0, i], z_sems.at[1, i], dev(me_t, xor(z, nz - 1 - i), y, c)
         )
 
-    def reduced(i):
-        total = quad_send[i, me_t, y].astype(f32)
-        for dt, dy in quad_slots:
-            quad_copy(i, dt, dy).wait_recv()
-            total = total + quad_recv[i, dt * nb + dy - 1].astype(f32)
+    def over_y(i):
+        total = y_send[i, y].astype(f32)
+        for dy in y_peers:
+            y_copy(i, dy).wait_recv()
+            total = total + y_recv[i, dy - 1].astype(f32)
+        total = total.astype(bf16)
+        for t in range(n_t):
+            x_send[i, t] = total[:, t * cols : (t + 1) * cols]
+        for s in tensor_peers:
+            x_copy(i, s).start()
+
+    def over_x(i):
+        total = x_send[i, me_t].astype(f32)
+        for s in tensor_peers:
+            x_copy(i, s).wait_recv()
+            total = total + x_recv[i, s - 1].astype(f32)
         return total
-
-    def pass_on(i):
-        z_send[i] = reduced(i).astype(bf16)
-        z_copy(i).start()
 
     def project(k, step, ready):
         projected = 0.0
@@ -270,11 +274,10 @@
         low = lax.dot_general(
             projected, heads[...], (((0,), (0,)), ((), ())), preferred_element_type=f32
         ).astype(bf16)
-        for t in range(n_t):
-            for yy in range(nb):
-                quad_send[i, t, yy] = low[yy * cr : (yy + 1) * cr, t * cols : (t + 1) * cols]
-        for dt, dy in quad_slots:
-            quad_copy(i, dt, dy).start()
+        for yy in range(nb):
+            y_send[i, yy] = low[yy * cr : (yy + 1) * cr, :]
+        for dy in y_peers:
+            y_copy(i, dy).start()
 
     def arrive(j):
         tok_copy(j // (lw // 4)).wait_recv()
@@ -294,33 +297,39 @@
 
     def chunk(i, carry):
         low_rank(i, project(xor(z, nz - 1 - i), deep, lambda j: None))
+
+        @pl.when(i == RELAY0)
+        def _():
+            relay_z(0)
+
         return carry
 
     lax.fori_loop(1, nz, chunk, 0)
 
-    relay(0)
-    for i in range(nz - 1):
-        pass_on(i)
-    fill(ra, rb, 2 * q * 2 * own_rows, 2 * low_rows, True)
     def back_rows(h, carry):
         place = pl.ds(pl.multiple_of(h * low_rows, low_rows), low_rows)
         for k in range(nz):
             back[k, place, :] = tables(ra, rb, h, k)
         return carry
 
-    lax.fori_loop(0, back.shape[1] // low_rows, back_rows, 0)
-    loads[4].wait()
-    lane = min(128, 2 * own_rows)
-    for b in range(2 * own_rows // lane):
-        at = slice(b * lane, (b + 1) * lane)
-        row = (2 * jnp.where(c == 0, sgn_b[0:1, at], sgn_b[1:2, at]) - 1).astype(f32)
-        sgn_col[b * lane : (b + 1) * lane, :] = jnp.broadcast_to(row, (128, lane)).T
-    loads[7].wait()
-    for s in tensor_peers:
-        hf_copy(s).wait_recv()
-    for t in range(n_t):
-        for m in range(2):
-            pair_heads[t, :, m * cols : (m + 1) * cols] = hc_all[t, :, m].reshape(2 * rows, cols)
+    def fill_back():
+        fill(ra, rb, 2 * q * 2 * own_rows, 2 * low_rows, True)
+        for s in tensor_peers:
+            hf_copy(s).wait_recv()
+        for t in range(n_t):
+            for m in range(2):
+                pair_heads[t, :, m * cols : (m + 1) * cols] = hc_all[t, :, m].reshape(2 * rows, cols)
+
+    def build_back():
+        lax.fori_loop(0, back.shape[1] // low_rows, back_rows, 0)
+
+    def column_signs():
+        loads[4].wait()
+        lane = min(128, 2 * own_rows)
+        for b in range(2 * own_rows // lane):
+            at = slice(b * lane, (b + 1) * lane)
+            row = (2 * jnp.where(c == 0, sgn_b[0:1, at], sgn_b[1:2, at]) - 1).astype(f32)
+            sgn_col[b * lane : (b + 1) * lane, :] = jnp.broadcast_to(row, (128, lane)).T
 
     def own_gradient(j, carry):
         place = pl.ds(pl.multiple_of(j * wide, wide), wide)
@@ -328,15 +337,27 @@
         g_acc[:, place] = dot_last(pair_heads[me_t], w)
         return carry
 
+    fillers = {0: fill_back, 1: build_back, 2: column_signs}
+    for i in range(nz):
+        over_y(i)
+        if i == 1:
+            relay_z(1)
+        if i in fillers:
+            fillers[i]()
+        if i:
+            z_send[i - 1] = over_x(i - 1).astype(bf16)
+            z_copy(i - 1).start()
+    relay_y(0)
+    relay_y(1)
+    loads[7].wait()
     lax.fori_loop(0, half // wide, own_gradient, 0)
-    relay(1)
     for i in (5, 6):
         loads[i].wait()
     for i in (1, 2):
         early[i].wait_recv()
 
-    total = reduced(nz - 1)
-    for k in range(2, nb + 1):
+    total = over_x(nz - 1)
+    for k in range(2, 2 * nb):
         fetch(k)
     for i in range(nz - 1):
         z_copy(i).wait_recv()
@@ -369,17 +390,17 @@
     for copy in res_copies:
         copy.start()
 
-    forward()
     for s in range(1, nz):
         ag_copy(s, 0).wait_recv()
         for dy in range(1, nb):
             ag_copy(s, dy).start()
     for s in tensor_peers:
-        for dy in y_peers:
-            wy_copy(s, 1, dy).wait_recv()
-            wx_copy(s, 1 + dy).wait_recv()
-        for k in range(nb + 1):
-            wz_copy(s, k).wait_recv()
+        for k in range(2, 2 * nb):
+            wx_copy(s, k).wait_recv()
+        for p in range(2):
+            wz_copy(s, p).wait_recv()
+            for dy in y_peers:
+                wy_copy(s, p, dy).wait_recv()
 
     def add_gradient(j, carry):
         place = pl.ds(pl.multiple_of(j * wide, wide), wide)
@@ -436,16 +457,18 @@
         for k in range(2):
             hx_copy(s, k).wait_send()
         hf_copy(s).wait_send()
-        for k in range(nb + 1):
+        for k in range(2 * nb):
             wx_copy(s, k).wait_send()
-            wz_copy(s, k).wait_send()
+        for p in range(2):
+            wz_copy(s, p).wait_send()
+            for dy in y_peers:
+                wy_copy(s, p, dy).wait_send()
+
+    def sent(i, carry):
         for dy in y_peers:
-            for p in range(2):
-                wy_copy(s, p, dy).wait_send()
-
-    def sent(i, carry):
-        for dt, dy in quad_slots:
-            quad_copy(i, dt, dy).wait_send()
+            y_copy(i, dy).wait_send()
+        for s in tensor_peers:
+            x_copy(i, s).wait_send()
         return carry
 
     lax.fori_loop(0, nz, sent, 0)
@@ -487,7 +510,6 @@
     low_rows = min(128, 2 * own_rows)
     up8 = lambda n: -(-n // 8) * 8
     half = lw // 2
-    group = n_t * nb - 1
 
     anywhere, vmem = pl.BlockSpec(memory_space=pltpu.HBM), pl.BlockSpec(memory_space=pltpu.VMEM)
     dma = pltpu.SemaphoreType.DMA
@@ -512,7 +534,8 @@
             V((nz, up8(2 * own_rows // low_rows), zr), f32), V((nz, up8(2 * own_rows // low_rows), zr), f32),
             V((nz, 2 * own_rows, zr), bf16), V((2 * own_rows, 128), f32),
             V((n_t, 2, 2, rows, cols), bf16), V((2 * rows, n_t * cols), bf16), V((n_t, 2 * rows, 2 * cols), bf16),
-            V((nz, n_t, nb, cr, cols), bf16), V((nz, group, cr, cols), bf16),
+            V((nz, nb, cr, n_t * cols), bf16), V((nz, nb - 1, cr, n_t * cols), bf16),
+            V((nz, n_t, cr, cols), bf16), V((nz, n_t - 1, cr, cols), bf16),
             V((nz, cr, cols), bf16), V((nz, cr, cols), bf16),
             V((2, 2, own, cols), f32), V((2, 2, own, cols), f32), V((2, own, cols), f32),
             V((nz * nb, cr, cols), bf16), V((2 * own_rows, cols), f32),
@@ -520,8 +543,8 @@
             V((2, half, cols), bf16), V((n_t - 1, 2, half, cols), bf16),
             V((2 * rows, half), f32), V((rows, half), bf16), V((rows, half), bf16),
             dma((8,)), dma((2, 7)), dma((2, 4)), dma((2, n_t - 1, 2)), dma((2, n_t - 1)),
-            dma((2, n_t - 1, nb + 1)), dma((2, n_t - 1, 2, nb - 1)), dma((2, n_t - 1, nb + 1)),
-            dma((2, nz, group)), dma((2, nz)), dma((2, nz, nb)),
+            dma((2, n_t - 1, 2 * nb)), dma((2, n_t - 1, 2, nb - 1)), dma((2, n_t - 1, 2)),
+            dma((2, nz, nb - 1)), dma((2, nz, n_t - 1)), dma((2, nz)), dma((2, nz, nb)),
         ],
         compiler_params=pltpu.CompilerParams(
             collective_id=0, has_side_effects=True, vmem_limit_bytes=48 * 1024 * 1024

time: 36.4 us -> 34.6 us (0.951)
  Pallas kernels: 35.6 us -> 33.7 us
    pallas_call x1, Pallas kernels: 34.5 us -> 32.6 us  [shards(): pl.pallas_call(functools.partial(main_kernel, plan), out_shape=(jax.Shape...]
where the time goes in v4:
time: 34.6 us; the launch traced here: 34.4 us
  Pallas kernels  33.7 us (97%)
  between operations  0.64 us (2%)
    pallas_call x1, Pallas kernels, shards(): pl.pallas_call(functools.partial(main_kernel, plan), out_shape=(jax.Shape...  32.6 us
    pallas_call x1, Pallas kernels, shards(): pl.pallas_call(write_kernel, out_shape=(jax.ShapeDtypeStruct((rows, lw),...  1.13 us

profile of v4, /device:TPU:0, one launch (start us, length us, event | category | flops | bytes accessed | tf_op | source)
XLA Modules:
  0.0 34.4 jit_solution(18363455216330719552)
XLA Ops:
  0.6 32.6 %shard_map.102 = (bf16[2,128,2048]{2,1,0:T(8,128)(2,1)S(1)}, f32[2,64,128]{2,1,0:T(8,128)S(1)}, f32[2,64,128]{2,1,0:T(8,128)S(1)}, bf16[2,512,128]{2,1,0:T(8,128)(2,1)S(1)}) custom-call(bf16[128,4096]{1,0:T(8,128)(2,1)} %tok_ref.1, bf16[2,8192,128]{2,1,0:T(8,128)(2,1)} %w_ref.1, bf16[2,128,128]{2,1,0:T(8,128)(2,1)} %hc_ref.1, s32[2,1024]{1,0:T(2,128)} %freq_ref.1, ...), custom_call_target="tpu_custom_call" | custom-call | tf_op jit(solution)/shard_map/pallas_call | solution.py:519
  33.2 1.1 %shard_map.103 = (bf16[128,4096]{1,0:T(8,128)(2,1)}, f32[2,64,128]{2,1,0:T(8,128)}, f32[2,64,128]{2,1,0:T(8,128)}, bf16[2,512,128]{2,1,0:T(8,128)(2,1)}) custom-call(bf16[2,128,2048]{2,1,0:T(8,128)(2,1)S(1)} %get-tuple-element.8.ig, f32[2,64,128]{2,1,0:T(8,128)S(1)} %get-tuple-element.9.nf, f32[2,64,128]{2,1,0:T(8,128)S(1)} %get-tuple-element.10.ns, ...), custom_call_target="tpu_custom_call" | custom-call | tf_op jit(solution)/shard_map/pallas_call | solution.py:553

commit v5 on v4

--- a/solution.py
+++ b/solution.py
@@ -13,6 +13,7 @@
 epsilon = 1e-08
 bf16, f32 = jnp.bfloat16, jnp.float32
 RELAY0 = 2
+DIRECT = 4
 
 
 def wrap(value, period):
@@ -43,9 +44,9 @@
     tok_ref, w_ref, hc_ref, freq_ref, sign_ref, first_ref, second_ref,
     ig_ref, nf_ref, ns_ref, full_ref,
     tok_all, tok_s, freq, sgn, sgn_b, cb, sb, ca, sa, ra, rb, back, sgn_col,
-    hc_all, heads, pair_heads, y_send, y_recv, x_send, x_recv, z_send, z_recv, mom, res, res_in, dirs, facc,
+    hc_all, heads, pair_heads, y_send, y_recv, x_send, x_recv, d_recv, z_send, z_recv, mom, res, res_in, dirs, facc,
     f_send, f_recv, w_own, wp, g_acc, g_send, g_recv,
-    loc, core_sems, tok_sems, hx_sems, hf_sems, wx_sems, wy_sems, wz_sems, y_sems, x_sems, z_sems, ag_sems,
+    loc, core_sems, g_sems, tok_sems, hx_sems, hf_sems, wx_sems, wy_sems, wz_sems, y_sems, x_sems, d_sems, z_sems, ag_sems,
 ):
     n_t, nz, nb, low_rows, token_count, width = plan
     rows, lw = tok_all.shape[1], tok_all.shape[2]
@@ -59,6 +60,7 @@
     piece = part // 2
     wide = min(512, half)
     deep = min(2048, lw)
+    first_direct = max(0, nz - DIRECT)
     me_t, me_d = lax.axis_index("tensor"), lax.axis_index("dp")
     c, q = me_d % 2, me_d // 2
     y, z = q % nb, q // nb
@@ -102,6 +104,7 @@
         peers.append(dev(me_t, z, (y + dy) % nb, c))
     for dt in range(1, n_t):
         peers += [dev((me_t + dt) % n_t, z, y, c), dev((me_t + dt) % n_t, z, y, oc)]
+        peers += [dev((me_t + dt) % n_t, z, (y + dy) % nb, c) for dy in range(1, nb)]
     for s in range(1, nz):
         peers.append(dev(me_t, xor(z, s), y, c))
     for device in peers:
@@ -205,7 +208,6 @@
     for copy in early:
         copy.start()
     fetch(0)
-    fetch(1)
 
     fill(ca, sa, 2 * me_t * lw, 2 * low_rows, True)
 
@@ -242,6 +244,22 @@
         return remote(
             z_send.at[i], z_recv.at[i], z_sems.at[0, i], z_sems.at[1, i], dev(me_t, xor(z, nz - 1 - i), y, c)
         )
+
+    corners = [(dt, dy) for dt in range(n_t) for dy in range(nb) if dt or dy]
+
+    def corner_copy(i, dt, dy):
+        t, yy, slot = (me_t + dt) % n_t, (y + dy) % nb, dt * nb + dy - 1
+        return remote(
+            y_send.at[i, yy, :, pl.ds(pl.multiple_of(t * cols, 128), cols)], d_recv.at[i - first_direct, slot],
+            d_sems.at[0, i - first_direct, slot], d_sems.at[1, i - first_direct, slot], dev(t, z, yy, c),
+        )
+
+    def direct_sum(i):
+        total = y_send[i, y, :, pl.ds(pl.multiple_of(me_t * cols, 128), cols)].astype(f32)
+        for dt, dy in corners:
+            corner_copy(i, dt, dy).wait_recv()
+            total = total + d_recv[i - first_direct, dt * nb + dy - 1].astype(f32)
+        return total
 
     def over_y(i):
         total = y_send[i, y].astype(f32)
@@ -270,14 +288,18 @@
             projected = projected + jnp.dot(signed, basis, preferred_element_type=f32)
         return projected.astype(bf16)
 
-    def low_rank(i, projected):
+    def low_rank(i, projected, direct):
         low = lax.dot_general(
             projected, heads[...], (((0,), (0,)), ((), ())), preferred_element_type=f32
         ).astype(bf16)
         for yy in range(nb):
             y_send[i, yy] = low[yy * cr : (yy + 1) * cr, :]
-        for dy in y_peers:
-            y_copy(i, dy).start()
+        if direct:
+            for dt, dy in sorted(corners, key=lambda at: at[0] * at[1] == 0):
+                corner_copy(i, dt, dy).start()
+        else:
+            for dy in y_peers:
+                y_copy(i, dy).start()
 
     def arrive(j):
         tok_copy(j // (lw // 4)).wait_recv()
@@ -291,20 +313,25 @@
             hx_copy(s, k).wait_recv()
     for t in range(n_t):
         heads[:, t * cols : (t + 1) * cols] = hc_all[t, :, pl.ds(c, 1)].reshape(2 * rows, cols)
-    low_rank(0, projected)
+    low_rank(0, projected, first_direct == 0)
     for s in tensor_peers:
         hf_copy(s).start()
 
-    def chunk(i, carry):
-        low_rank(i, project(xor(z, nz - 1 - i), deep, lambda j: None))
-
-        @pl.when(i == RELAY0)
-        def _():
-            relay_z(0)
-
-        return carry
-
-    lax.fori_loop(1, nz, chunk, 0)
+    def chunks(start, stop, direct):
+        def chunk(i, carry):
+            low_rank(i, project(xor(z, nz - 1 - i), deep, lambda j: None), direct)
+
+            @pl.when(i == RELAY0)
+            def _():
+                relay_z(0)
+
+            return carry
+
+        lax.fori_loop(start, stop, chunk, 0)
+
+    if first_direct > 1:
+        chunks(1, first_direct, False)
+    chunks(max(1, first_direct), nz, True)
 
     def back_rows(h, carry):
         place = pl.ds(pl.multiple_of(h * low_rows, low_rows), low_rows)
@@ -338,17 +365,25 @@
         return carry
 
     fillers = {0: fill_back, 1: build_back, 2: column_signs}
-    for i in range(nz):
-        over_y(i)
-        if i == 1:
-            relay_z(1)
+
+    def to_z(i, total):
+        z_send[i] = total.astype(bf16)
+        z_copy(i).start()
+
+    for i in range(nz - 1):
+        if i < first_direct:
+            over_y(i)
         if i in fillers:
             fillers[i]()
-        if i:
-            z_send[i - 1] = over_x(i - 1).astype(bf16)
-            z_copy(i - 1).start()
+        if 0 < i <= first_direct:
+            to_z(i - 1, over_x(i - 1))
+        if i >= first_direct:
+            to_z(i, direct_sum(i))
+        if i == nz - 2:
+            fetch(1)
+    if first_direct == nz - 1:
+        to_z(nz - 2, over_x(nz - 2))
     relay_y(0)
-    relay_y(1)
     loads[7].wait()
     lax.fori_loop(0, half // wide, own_gradient, 0)
     for i in (5, 6):
@@ -356,7 +391,7 @@
     for i in (1, 2):
         early[i].wait_recv()
 
-    total = over_x(nz - 1)
+    total = direct_sum(nz - 1)
     for k in range(2, 2 * nb):
         fetch(k)
     for i in range(nz - 1):
@@ -394,30 +429,48 @@
         ag_copy(s, 0).wait_recv()
         for dy in range(1, nb):
             ag_copy(s, dy).start()
-    for s in tensor_peers:
-        for k in range(2, 2 * nb):
-            wx_copy(s, k).wait_recv()
-        for p in range(2):
-            wz_copy(s, p).wait_recv()
-            for dy in y_peers:
-                wy_copy(s, p, dy).wait_recv()
-
-    def add_gradient(j, carry):
-        place = pl.ds(pl.multiple_of(j * wide, wide), wide)
+        if s == min(1, nz - 1):
+            relay_z(1)
+            relay_y(1)
+    def g_copy(k, place):
+        return remote(g_send.at[:, place], g_recv.at[:, place], g_sems.at[0, k], g_sems.at[1, k], other)
+
+    def add_gradient(k, place):
         value = g_acc[:, place]
-        for s in range(1, n_t):
+        for s in tensor_peers:
             w = jnp.concatenate([wp[s - 1, m, place, :] for m in range(2)], axis=1)
             value = value + dot_last(pair_heads[(me_t + n_t - s) % n_t], w)
         g_acc[:, place] = value
         g_send[:, place] = g_acc[pl.ds(pl.multiple_of(oc * rows, rows), rows), place].astype(bf16)
         mine = g_acc[pl.ds(pl.multiple_of(c * rows, rows), rows), place].astype(bf16)
         ig_ref[pl.ds(c, 1), :, place] = mine[None]
-        return carry
-
-    lax.fori_loop(0, half // wide, add_gradient, 0)
-    g_copy = remote(g_send, g_recv, core_sems.at[0, 6], core_sems.at[1, 6], other)
-    g_copy.start()
-
+        g_copy(k, place).start()
+
+    pieces = [(y, zl, 0), (y, 1 - zl, 0)] + [((y + nb - dy) % nb, zl, 0) for dy in y_peers]
+    pieces += [(y, zl, 1), (y, 1 - zl, 1)] + [((y + nb - dy) % nb, zl, 1) for dy in y_peers]
+    pieces += [((y + dy) % nb, 1 - zl, p) for dy in y_peers for p in range(2)]
+    fine = piece % 128 == 0
+    places = [pl.ds(pl.multiple_of(rows_of(*at), 128), piece) for at in pieces] if fine else [slice(0, half)]
+
+    def early_pieces(p):
+        for s in tensor_peers:
+            wz_copy(s, p).wait_recv()
+            for dy in y_peers:
+                wy_copy(s, p, dy).wait_recv()
+        if fine:
+            for k in range(p * (nb + 1), (p + 1) * (nb + 1)):
+                add_gradient(k, places[k])
+
+    def late_pieces():
+        for j in range(2 * nb - 2):
+            for s in tensor_peers:
+                wx_copy(s, 2 + j).wait_recv()
+            if fine:
+                add_gradient(2 * (nb + 1) + j, places[2 * (nb + 1) + j])
+        if not fine:
+            add_gradient(0, places[0])
+
+    early_pieces(0)
     nf_ref[pl.ds(c, 1)] = res[0, pl.ds(c, 1)]
     ns_ref[pl.ds(c, 1)] = res[1, pl.ds(c, 1)]
     for copy in res_copies:
@@ -443,15 +496,20 @@
     f_copy = remote(f_send, f_recv, core_sems.at[0, 5], core_sems.at[1, 5], other)
     f_copy.start()
     full_ref[pl.ds(c, 1)] = finished(c)[None]
-
-    for copy in (g_copy, f_copy):
-        copy.wait_recv()
+    early_pieces(1)
+    late_pieces()
+
+    f_copy.wait_recv()
+    for k, place in enumerate(places):
+        g_copy(k, place).wait_recv()
     ig_ref[pl.ds(oc, 1)] = g_recv[...][None]
     full_ref[pl.ds(oc, 1)] = f_recv[...][None]
 
     for p in range(4):
         tok_copy(p).wait_send()
-    for copy in early + res_copies + [f_copy, g_copy]:
+    for k, place in enumerate(places):
+        g_copy(k, place).wait_send()
+    for copy in early + res_copies + [f_copy]:
         copy.wait_send()
     for s in range(1, n_t):
         for k in range(2):
@@ -471,7 +529,14 @@
             x_copy(i, s).wait_send()
         return carry
 
-    lax.fori_loop(0, nz, sent, 0)
+    def sent_direct(i, carry):
+        for dt, dy in corners:
+            corner_copy(i, dt, dy).wait_send()
+        return carry
+
+    if first_direct:
+        lax.fori_loop(0, first_direct, sent, 0)
+    lax.fori_loop(first_direct, nz, sent_direct, 0)
     for i in range(nz - 1):
         z_copy(i).wait_send()
     for s in range(nz):
@@ -536,15 +601,17 @@
             V((n_t, 2, 2, rows, cols), bf16), V((2 * rows, n_t * cols), bf16), V((n_t, 2 * rows, 2 * cols), bf16),
             V((nz, nb, cr, n_t * cols), bf16), V((nz, nb - 1, cr, n_t * cols), bf16),
             V((nz, n_t, cr, cols), bf16), V((nz, n_t - 1, cr, cols), bf16),
+            V((min(DIRECT, nz), n_t * nb - 1, cr, cols), bf16),
             V((nz, cr, cols), bf16), V((nz, cr, cols), bf16),
             V((2, 2, own, cols), f32), V((2, 2, own, cols), f32), V((2, own, cols), f32),
             V((nz * nb, cr, cols), bf16), V((2 * own_rows, cols), f32),
             V((own_rows, cols), bf16), V((own_rows, cols), bf16),
             V((2, half, cols), bf16), V((n_t - 1, 2, half, cols), bf16),
             V((2 * rows, half), f32), V((rows, half), bf16), V((rows, half), bf16),
-            dma((8,)), dma((2, 7)), dma((2, 4)), dma((2, n_t - 1, 2)), dma((2, n_t - 1)),
+            dma((8,)), dma((2, 6)), dma((2, 4 * nb)), dma((2, 4)), dma((2, n_t - 1, 2)), dma((2, n_t - 1)),
             dma((2, n_t - 1, 2 * nb)), dma((2, n_t - 1, 2, nb - 1)), dma((2, n_t - 1, 2)),
-            dma((2, nz, nb - 1)), dma((2, nz, n_t - 1)), dma((2, nz)), dma((2, nz, nb)),
+            dma((2, nz, nb - 1)), dma((2, nz, n_t - 1)),
+            dma((2, min(DIRECT, nz), n_t * nb - 1)), dma((2, nz)), dma((2, nz, nb)),
         ],
         compiler_params=pltpu.CompilerParams(
             collective_id=0, has_side_effects=True, vmem_limit_bytes=48 * 1024 * 1024

time: 34.6 us -> 34.3 us (level)
  no operation moved by 1% of the time
where the time goes in v5:
time: 34.3 us; the launch traced here: 34.1 us
  Pallas kernels  33.5 us (98%)
  between operations  0.64 us (2%)
    pallas_call x1, Pallas kernels, shards(): pl.pallas_call(functools.partial(main_kernel, plan), out_shape=(jax.Shape...  32.4 us
    pallas_call x1, Pallas kernels, shards(): pl.pallas_call(write_kernel, out_shape=(jax.ShapeDtypeStruct((rows, lw),...  1.13 us

profile of v5, /device:TPU:0, one launch (start us, length us, event | category | flops | bytes accessed | tf_op | source)
XLA Modules:
  0.0 34.1 jit_solution(7837580046909617594)
XLA Ops:
  0.6 32.4 %shard_map.102 = (bf16[2,128,2048]{2,1,0:T(8,128)(2,1)S(1)}, f32[2,64,128]{2,1,0:T(8,128)S(1)}, f32[2,64,128]{2,1,0:T(8,128)S(1)}, bf16[2,512,128]{2,1,0:T(8,128)(2,1)S(1)}) custom-call(bf16[128,4096]{1,0:T(8,128)(2,1)} %tok_ref.1, bf16[2,8192,128]{2,1,0:T(8,128)(2,1)} %w_ref.1, bf16[2,128,128]{2,1,0:T(8,128)(2,1)} %hc_ref.1, s32[2,1024]{1,0:T(2,128)} %freq_ref.1, ...), custom_call_target="tpu_custom_call" | custom-call | tf_op jit(solution)/shard_map/pallas_call | solution.py:584
  33.0 1.1 %shard_map.103 = (bf16[128,4096]{1,0:T(8,128)(2,1)}, f32[2,64,128]{2,1,0:T(8,128)}, f32[2,64,128]{2,1,0:T(8,128)}, bf16[2,512,128]{2,1,0:T(8,128)(2,1)}) custom-call(bf16[2,128,2048]{2,1,0:T(8,128)(2,1)S(1)} %get-tuple-element.8.ig, f32[2,64,128]{2,1,0:T(8,128)S(1)} %get-tuple-element.9.nf, f32[2,64,128]{2,1,0:T(8,128)S(1)} %get-tuple-element.10.ns, ...), custom_call_target="tpu_custom_call" | custom-call | tf_op jit(solution)/shard_map/pallas_call | solution.py:620

commit v6 on v5

--- a/solution.py
+++ b/solution.py
@@ -364,6 +364,7 @@
         g_acc[:, place] = dot_last(pair_heads[me_t], w)
         return carry
 
+    fetch(1)
     fillers = {0: fill_back, 1: build_back, 2: column_signs}
 
     def to_z(i, total):
@@ -379,8 +380,6 @@
             to_z(i - 1, over_x(i - 1))
         if i >= first_direct:
             to_z(i, direct_sum(i))
-        if i == nz - 2:
-            fetch(1)
     if first_direct == nz - 1:
         to_z(nz - 2, over_x(nz - 2))
     relay_y(0)
@@ -424,14 +423,13 @@
     ]
     for copy in res_copies:
         copy.start()
+    relay_z(1)
+    relay_y(1)
 
     for s in range(1, nz):
         ag_copy(s, 0).wait_recv()
         for dy in range(1, nb):
             ag_copy(s, dy).start()
-        if s == min(1, nz - 1):
-            relay_z(1)
-            relay_y(1)
     def g_copy(k, place):
         return remote(g_send.at[:, place], g_recv.at[:, place], g_sems.at[0, k], g_sems.at[1, k], other)
 
@@ -477,6 +475,7 @@
         copy.wait_recv()
     nf_ref[pl.ds(oc, 1)] = res_in[0][None]
     ns_ref[pl.ds(oc, 1)] = res_in[1][None]
+    early_pieces(1)
     facc[...] = jnp.zeros_like(facc)
     for s in range(nz):
         for dy in range(1, nb):
@@ -496,7 +495,6 @@
     f_copy = remote(f_send, f_recv, core_sems.at[0, 5], core_sems.at[1, 5], other)
     f_copy.start()
     full_ref[pl.ds(c, 1)] = finished(c)[None]
-    early_pieces(1)
     late_pieces()
 
     f_copy.wait_recv()

time: 34.3 us -> 32.7 us (0.953)
  Pallas kernels: 33.5 us -> 31.9 us
    pallas_call x1, Pallas kernels: 32.4 us -> 30.8 us  [shards(): pl.pallas_call(functools.partial(main_kernel, plan), out_shape=(jax.Shape...]
where the time goes in v6:
time: 32.7 us; the launch traced here: 32.5 us
  Pallas kernels  31.9 us (98%)
  between operations  0.64 us (2%)
    pallas_call x1, Pallas kernels, shards(): pl.pallas_call(functools.partial(main_kernel, plan), out_shape=(jax.Shape...  30.8 us
    pallas_call x1, Pallas kernels, shards(): pl.pallas_call(write_kernel, out_shape=(jax.ShapeDtypeStruct((rows, lw),...  1.13 us

profile of v6, /device:TPU:0, one launch (start us, length us, event | category | flops | bytes accessed | tf_op | source)
XLA Modules:
  0.0 32.5 jit_solution(1607935970301017612)
XLA Ops:
  0.6 30.8 %shard_map.102 = (bf16[2,128,2048]{2,1,0:T(8,128)(2,1)S(1)}, f32[2,64,128]{2,1,0:T(8,128)S(1)}, f32[2,64,128]{2,1,0:T(8,128)S(1)}, bf16[2,512,128]{2,1,0:T(8,128)(2,1)S(1)}) custom-call(bf16[128,4096]{1,0:T(8,128)(2,1)} %tok_ref.1, bf16[2,8192,128]{2,1,0:T(8,128)(2,1)} %w_ref.1, bf16[2,128,128]{2,1,0:T(8,128)(2,1)} %hc_ref.1, s32[2,1024]{1,0:T(2,128)} %freq_ref.1, ...), custom_call_target="tpu_custom_call" | custom-call | tf_op jit(solution)/shard_map/pallas_call | solution.py:582
  31.4 1.1 %shard_map.103 = (bf16[128,4096]{1,0:T(8,128)(2,1)}, f32[2,64,128]{2,1,0:T(8,128)}, f32[2,64,128]{2,1,0:T(8,128)}, bf16[2,512,128]{2,1,0:T(8,128)(2,1)}) custom-call(bf16[2,128,2048]{2,1,0:T(8,128)(2,1)S(1)} %get-tuple-element.8.ig, f32[2,64,128]{2,1,0:T(8,128)S(1)} %get-tuple-element.9.nf, f32[2,64,128]{2,1,0:T(8,128)S(1)} %get-tuple-element.10.ns, ...), custom_call_target="tpu_custom_call" | custom-call | tf_op jit(solution)/shard_map/pallas_call | solution.py:618

commit v7 on v6

--- a/solution.py
+++ b/solution.py
@@ -482,7 +482,12 @@
             ag_copy(s, dy).wait_recv()
         zz = xor(z, s)
         block = dirs[pl.ds(zz * nb, nb)].reshape(zr, cols)
-        facc[...] += jnp.dot(back[zz], block, preferred_element_type=f32)
+        if s < nz - 1:
+            facc[...] += jnp.dot(back[zz], block, preferred_element_type=f32)
+
+    def last_rows(k):
+        place = pl.ds(pl.multiple_of(k * own_rows, own_rows), own_rows)
+        facc[place, :] += jnp.dot(back[zz, place, :], block, preferred_element_type=f32)
 
     def finished(k):
         place = pl.ds(pl.multiple_of(k * own_rows, own_rows), own_rows)
@@ -491,9 +496,11 @@
             [value[:, j : j + 128] * signs for j in range(0, cols, 128)], axis=1
         ).astype(bf16)
 
+    last_rows(oc)
     f_send[...] = finished(oc)
     f_copy = remote(f_send, f_recv, core_sems.at[0, 5], core_sems.at[1, 5], other)
     f_copy.start()
+    last_rows(c)
     full_ref[pl.ds(c, 1)] = finished(c)[None]
     late_pieces()
 

time: 32.7 us -> 32.8 us (level)
  no operation moved by 1% of the time
where the time goes in v7:
time: 32.8 us; the launch traced here: 32.6 us
  Pallas kernels  32 us (98%)
  between operations  0.64 us (2%)
    pallas_call x1, Pallas kernels, shards(): pl.pallas_call(functools.partial(main_kernel, plan), out_shape=(jax.Shape...  30.9 us
    pallas_call x1, Pallas kernels, shards(): pl.pallas_call(write_kernel, out_shape=(jax.ShapeDtypeStruct((rows, lw),...  1.13 us

profile of v7, /device:TPU:0, one launch (start us, length us, event | category | flops | bytes accessed | tf_op | source)
XLA Modules:
  0.0 32.6 jit_solution(8636639442398859155)
XLA Ops:
  0.6 30.9 %shard_map.102 = (bf16[2,128,2048]{2,1,0:T(8,128)(2,1)S(1)}, f32[2,64,128]{2,1,0:T(8,128)S(1)}, f32[2,64,128]{2,1,0:T(8,128)S(1)}, bf16[2,512,128]{2,1,0:T(8,128)(2,1)S(1)}) custom-call(bf16[128,4096]{1,0:T(8,128)(2,1)} %tok_ref.1, bf16[2,8192,128]{2,1,0:T(8,128)(2,1)} %w_ref.1, bf16[2,128,128]{2,1,0:T(8,128)(2,1)} %hc_ref.1, s32[2,1024]{1,0:T(2,128)} %freq_ref.1, ...), custom_call_target="tpu_custom_call" | custom-call | tf_op jit(solution)/shard_map/pallas_call | solution.py:589
  31.5 1.1 %shard_map.103 = (bf16[128,4096]{1,0:T(8,128)(2,1)}, f32[2,64,128]{2,1,0:T(8,128)}, f32[2,64,128]{2,1,0:T(8,128)}, bf16[2,512,128]{2,1,0:T(8,128)(2,1)}) custom-call(bf16[2,128,2048]{2,1,0:T(8,128)(2,1)S(1)} %get-tuple-element.8.ig, f32[2,64,128]{2,1,0:T(8,128)S(1)} %get-tuple-element.9.nf, f32[2,64,128]{2,1,0:T(8,128)S(1)} %get-tuple-element.10.ns, ...), custom_call_target="tpu_custom_call" | custom-call | tf_op jit(solution)/shard_map/pallas_call | solution.py:625
